TPU v7x, 32 devices: a whole 2x2x4 slice. The times are simulated.
32 devices in a mesh: groups: 2 (over x), expert: 16 (over z, y, core).
Axes of the slice: x: 2, y: 2, z: 4, core: 2. Of those that a mesh axis runs over, the one named last changes fastest.
Arguments:
- hidden_in: bfloat16 [256, 4096], P(('groups', 'expert')), parts along dimension 0, may hold values from -6 to 6
- queries: bfloat16 [256, 4096], P(('groups', 'expert')), parts along dimension 0, may hold values from -8 to 8
- decode_key_value: bfloat16 [256, 2, 256], P(('groups', 'expert')), parts along dimension 0, may hold values from -6 to 6
- local_kv: bfloat16 [1024, 2, 16, 256], P(('groups', 'expert')), parts along dimension 0, may hold values from -8 to 8
- page_table: int32 [256, 16], P(('groups', 'expert')), parts along dimension 0, may hold values from 0 to 31
- seq_blocks: int32 [256], P(('groups', 'expert')), parts along dimension 0, may hold values from 1 to 16
- prompt_kv: bfloat16 [32, 16, 2, 16, 256], P(('groups', 'expert')), parts along dimension 0, may hold values from -8 to 8
- prompt_owner: int32 [32], P('groups'), parts along dimension 0, may hold values from 0 to 15, as said below
- prompt_pages: int32 [32], P('groups'), parts along dimension 0, may hold values from 1 to 16
- norm_gain: float32 [4096], replicated, may hold values from 0.5 to 1.5
- router: bfloat16 [4096, 8], replicated, may hold values from -0.09375 to 0.09375
- w_gate: bfloat16 [16, 4096, 384], P('expert'), may hold values from -0.09375 to 0.09375
- w_up: bfloat16 [16, 4096, 384], P('expert'), may hold values from -0.09375 to 0.09375
- w_down: bfloat16 [16, 384, 4096], P('expert'), may hold values from -0.21875 to 0.21875
- route_ids: int32 [256, 8], P(('groups', 'expert')), parts along dimension 0, may hold values from 0 to 7, as said below
Outputs:
- layer_out: bfloat16 [256, 4096], P(('groups', 'expert')), parts along dimension 0
There are 2 independent parts, one for each index of `groups`. A program takes and returns all parts, laid end to end along the dimension named above; an argument that names none is the same for every part. Nothing has to cross between parts.
Inputs may be any that keep to these rules, and one draw needn't show every extreme that they name: `prompt_owner`: each device is named by at most 2 prompts, and by exactly 2 for some of the devices. `route_ids`: each row names 8 different experts; among the rows of one device no expert is named more than 8 times, a bound that some block reaches. `page_table`: indices among the pages of the sequence's own device.
All inputs are finite; a program needn't handle non-finite values.
Results may differ from a plain program's by a relative error of at most 0.0056.
Values may be sent and summed in bfloat16 or wider, within the bound.
A program may use at most 128 MiB of HBM per device.

v0:
```python
import functools
import math

import jax
import jax.numpy as jnp
from jax import lax
from jax.experimental import pallas as pl
from jax.experimental.pallas import tpu as pltpu
from jax.sharding import PartitionSpec as P

D = 4096
QUERY_HEADS = 32
KEY_VALUE_HEADS = 2
HEAD_SIZE = 128
PAGE_TOKENS = 16
TOPK = 8
MAXB = 16
MAXP = 2


norm_eps = 1e-06
masked_score = -1e30


def partner(x, axis, apart):
    return lax.ppermute(x, axis, [(i, i ^ 1 << apart) for i in range(lax.axis_size(axis))])


def attend(rows_of_queries, rows_of_keys, rows_of_values, allowed, token_own_key, token_own_value):
    decode_tokens = rows_of_queries.shape[0]
    heads_of_queries = rows_of_queries.reshape(
        decode_tokens, KEY_VALUE_HEADS, QUERY_HEADS // KEY_VALUE_HEADS, HEAD_SIZE
    )
    heads_of_keys = rows_of_keys.reshape(decode_tokens, -1, KEY_VALUE_HEADS, HEAD_SIZE)
    heads_of_values = rows_of_values.reshape(decode_tokens, -1, KEY_VALUE_HEADS, HEAD_SIZE)
    scale_for_scores = 1.0 / math.sqrt(HEAD_SIZE)
    allowed_mask = allowed[:, None, None, :]
    scores = (
        jnp.einsum(
            "tkgd,tlkd->tkgl", heads_of_queries, heads_of_keys, preferred_element_type=jnp.float32
        )
        * scale_for_scores
    )
    scores = jnp.where(allowed_mask, scores, masked_score)
    token_own_score = (
        jnp.einsum(
            "xejp,xep->xej",
            heads_of_queries,
            token_own_key.reshape(decode_tokens, KEY_VALUE_HEADS, HEAD_SIZE),
            preferred_element_type=jnp.float32,
        )
        * scale_for_scores
    )
    peak = jnp.maximum(jnp.max(scores, -1), token_own_score)
    weights = jnp.where(allowed_mask, jnp.exp(scores - peak[..., None]), 0.0)
    own_weight = jnp.exp(token_own_score - peak)
    denominator = jnp.sum(weights, -1) + own_weight
    probs = (weights / denominator[..., None]).astype(jnp.bfloat16)
    token_own_probability = (own_weight / denominator).astype(jnp.bfloat16)
    blended_noise = jnp.einsum(
        "tkgl,tlkd->tkgd", probs, heads_of_values, preferred_element_type=jnp.float32
    )
    blended_noise = blended_noise + token_own_probability.astype(jnp.float32)[
        ..., None
    ] * token_own_value.reshape(decode_tokens, KEY_VALUE_HEADS, 1, HEAD_SIZE).astype(jnp.float32)
    return blended_noise.reshape(decode_tokens, QUERY_HEADS * HEAD_SIZE).astype(jnp.bfloat16)


def routed(
    hidden_in,
    queries,
    decode_key_value,
    local_kv,
    page_table,
    seq_blocks,
    prompt_kv,
    prompt_owner,
    prompt_pages,
    norm_gain,
    router,
    w_gate,
    w_up,
    w_down,
    route_ids,
):
    devices = lax.axis_size("expert")
    position = lax.axis_index("expert")
    experts = devices // 2
    seq_dev = hidden_in.shape[0]
    key_value_width = KEY_VALUE_HEADS * HEAD_SIZE
    capacity = min(seq_dev, max(2, 2 * ((3 * seq_dev * TOPK + 2 * devices - 1) // (2 * devices))))
    half_cap = capacity // 2
    even_core = position % 2 == 0
    prompt_count = prompt_owner.shape[0]
    prompt_range = jnp.arange(prompt_count, dtype=jnp.int32)
    same_owner = prompt_owner[:, None] == prompt_owner[None, :]
    earlier = prompt_range[None, :] < prompt_range[:, None]
    arrival = jnp.sum((same_owner & earlier).astype(jnp.int32), 1)
    matching = (
        prompt_owner[None, None, :] == jnp.arange(devices, dtype=jnp.int32)[:, None, None]
    ) & (arrival[None, None, :] == jnp.arange(MAXP, dtype=jnp.int32)[None, :, None])
    chosen_prompt = jnp.sum(jnp.where(matching, prompt_range[None, None, :], 0), -1)
    occupied = jnp.any(matching, -1)
    own_picks = lax.dynamic_index_in_dim(chosen_prompt, position, 0, keepdims=False)
    own_occupied = lax.dynamic_index_in_dim(occupied, position, 0, keepdims=False)
    page_rows = prompt_kv[0]
    outgoing = jnp.take(page_rows, chosen_prompt.T.reshape(-1), axis=0).reshape(
        MAXP, devices, 2, PAGE_TOKENS, key_value_width
    )
    outgoing = jnp.where(occupied.T[:, :, None, None, None], outgoing, 0)
    arrived = lax.all_to_all(outgoing, "expert", split_axis=1, concat_axis=1, tiled=True)
    lengths = jnp.take(prompt_pages, own_picks)
    new_keys = arrived[:, :, 0].reshape(MAXP, devices * PAGE_TOKENS, key_value_width)
    new_values = arrived[:, :, 1].reshape(MAXP, devices * PAGE_TOKENS, key_value_width)
    new_allowed = (jnp.arange(devices * PAGE_TOKENS, dtype=jnp.int32) // PAGE_TOKENS)[
        None, :
    ] < lengths[:, None]
    fresh_rows = attend(
        queries[:MAXP],
        new_keys,
        new_values,
        new_allowed,
        decode_key_value[:MAXP, 0],
        decode_key_value[:MAXP, 1],
    )
    fetched = local_kv[page_table]
    old_keys = fetched[:, :, 0].reshape(seq_dev, MAXB * PAGE_TOKENS, key_value_width)
    old_values = fetched[:, :, 1].reshape(seq_dev, MAXB * PAGE_TOKENS, key_value_width)
    old_allowed = (jnp.arange(MAXB * PAGE_TOKENS, dtype=jnp.int32) // PAGE_TOKENS)[
        None, :
    ] < seq_blocks[:, None]
    old_out = attend(
        queries, old_keys, old_values, old_allowed, decode_key_value[:, 0], decode_key_value[:, 1]
    )
    new_count = jnp.sum(own_occupied.astype(jnp.int32))
    is_new = jnp.arange(MAXP, dtype=jnp.int32) < new_count
    attention = jnp.concatenate(
        [jnp.where(is_new[:, None], fresh_rows, old_out[:MAXP]), old_out[MAXP:]], 0
    )
    residual = (hidden_in.astype(jnp.float32) + attention.astype(jnp.float32)).astype(jnp.bfloat16)
    resid_wide = residual.astype(jnp.float32)
    normed = (
        resid_wide
        * lax.rsqrt(jnp.mean(resid_wide * resid_wide, -1, keepdims=True) + norm_eps)
        * norm_gain
    ).astype(jnp.bfloat16)
    logits = jnp.dot(normed, router, preferred_element_type=jnp.float32)
    expert_onehot = route_ids[:, :, None] == jnp.arange(experts, dtype=jnp.int32)[None, None, :]
    selected = jnp.sum(jnp.where(expert_onehot, logits[:, None, :], 0.0), -1)
    gate_weights = jax.nn.softmax(selected, -1)
    assigned = seq_dev * TOPK
    expert_ids = route_ids.reshape(assigned)
    chosen = (expert_ids[:, None] == jnp.arange(experts, dtype=jnp.int32)[None, :]).astype(
        jnp.int32
    )
    before = jnp.cumsum(chosen, 0) - chosen
    slot_rank = jnp.sum(before * chosen, 1)
    slot_index = expert_ids * capacity + slot_rank
    placing = slot_index[None, :] == jnp.arange(experts * capacity, dtype=jnp.int32)[:, None]
    selector = jnp.any(placing.reshape(experts * capacity, seq_dev, TOPK), -1).astype(jnp.bfloat16)
    gathered_rows = jnp.dot(selector, normed, preferred_element_type=jnp.float32).astype(
        jnp.bfloat16
    )
    outgoing_half = gathered_rows.reshape(devices, half_cap, D)
    own_half = lax.all_to_all(outgoing_half, "expert", split_axis=0, concat_axis=0, tiled=True)
    partner_half = partner(own_half, "expert", 0)
    received = jnp.where(
        even_core,
        jnp.concatenate([own_half, partner_half], 1),
        jnp.concatenate([partner_half, own_half], 1),
    )
    flattened = received.reshape(devices * capacity, D)
    gate_proj = jnp.dot(flattened, w_gate[0], preferred_element_type=jnp.float32)
    up_proj = jnp.dot(flattened, w_up[0], preferred_element_type=jnp.float32)
    activated = (jax.nn.silu(gate_proj) * up_proj).astype(jnp.bfloat16)
    partial_value = jnp.dot(activated, w_down[0], preferred_element_type=jnp.float32).reshape(
        devices, capacity, D
    )
    kept = jnp.where(even_core, partial_value[:, :half_cap], partial_value[:, half_cap:])
    handed = jnp.where(even_core, partial_value[:, half_cap:], partial_value[:, :half_cap])
    partner_part = partner(handed, "expert", 0)
    finished = (kept + partner_part).astype(jnp.bfloat16)
    returned = lax.all_to_all(finished, "expert", split_axis=0, concat_axis=0, tiled=True)
    expert_sum = returned.reshape(experts * capacity, D)
    picked = jnp.take(expert_sum, slot_index, axis=0).astype(jnp.float32).reshape(seq_dev, TOPK, D)
    expert_mix = jnp.sum(picked * gate_weights[:, :, None], 1)
    return (resid_wide + expert_mix).astype(jnp.bfloat16)


def layer_kernel(
    devices,
    owners,
    prompt_lengths,
    blocks,
    pages_hbm,
    q_hbm,
    dkv_hbm,
    table_hbm,
    kv_hbm,
    hidden_hbm,
    gain_hbm,
    router_hbm,
    ids_hbm,
    gate_hbm,
    up_hbm,
    down_hbm,
    out_ref,
    pages_ref,
    q_ref,
    dkv_ref,
    table_ref,
    kv_ref,
    hidden_ref,
    gain_ref,
    router_ref,
    ids_ref,
    w_gate,
    w_up,
    w_down,
    kv_send,
    kv_recv,
    attn,
    x_all,
    gates,
    part,
    core_recv,
    y_send,
    y_recv,
    z_send,
    z_recv,
    kept,
    in_sem,
    w_sem,
    kv_ssem,
    kv_rsem,
    x_ssem,
    x_rsem,
    c_sem,
    y_sem,
    zs_sem,
    zr_sem,
):
    f32, bf16 = jnp.float32, jnp.bfloat16
    me = lax.axis_index("expert")
    lines = devices // 4
    core, row, line = lax.rem(me, 2), lax.rem(me // 2, 2), me // 4
    seqs = hidden_ref.shape[0]
    group = QUERY_HEADS // KEY_VALUE_HEADS
    scale = 1.0 / math.sqrt(HEAD_SIZE)

    def device(at_line, at_row, at_core):
        return (at_line * 2 + at_row) * 2 + at_core

    def place(at_line, at_row, at_core):
        return (at_core * 2 + at_row) * lines + at_line

    def remote(src, dst, ssem, rsem, to):
        return pltpu.make_async_remote_copy(
            src_ref=src,
            dst_ref=dst,
            send_sem=ssem,
            recv_sem=rsem,
            device_id={"expert": to},
            device_id_type=pl.DeviceIdType.MESH,
        )

    loads = [
        pltpu.make_async_copy(a, b, in_sem.at[i])
        for i, (a, b) in enumerate(
            (
                (pages_hbm, pages_ref),
                (q_hbm, q_ref),
                (dkv_hbm, dkv_ref),
                (table_hbm, table_ref),
                (kv_hbm, kv_ref),
                (hidden_hbm, hidden_ref),
                (gain_hbm, gain_ref),
                (router_hbm, router_ref),
                (ids_hbm, ids_ref),
            )
        )
    ]
    weights = [
        pltpu.make_async_copy(a.at[0], b, w_sem.at[i])
        for i, (a, b) in enumerate(((gate_hbm, w_gate), (up_hbm, w_up), (down_hbm, w_down)))
    ]
    for copy in loads + weights:
        copy.start()

    barrier = pltpu.get_barrier_semaphore()

    def greet(k, carry):
        pl.semaphore_signal(
            barrier,
            inc=1,
            device_id={"expert": lax.rem(me + k, devices)},
            device_id_type=pl.DeviceIdType.MESH,
        )
        return carry

    lax.fori_loop(1, devices, greet, 0)

    prompts = owners.shape[0]

    def named(o):
        first, last, number = jnp.int32(0), jnp.int32(0), jnp.int32(0)
        for p in range(prompts):
            hit = owners[p] == o
            last = jnp.where(hit, p, last)
            number = number + hit.astype(jnp.int32)
        for p in reversed(range(prompts)):
            first = jnp.where(owners[p] == o, p, first)
        return (first, last), number

    def stage(o, carry):
        picks, _ = named(o)
        for r in range(MAXP):
            kv_send[o, r] = pages_ref[picks[r]]
        return carry

    loads[0].wait()
    lax.fori_loop(0, devices, stage, 0)
    own_picks, new_count = named(me)
    for r in range(MAXP):
        kv_recv[me, r] = pages_ref[own_picks[r]]
    pl.semaphore_wait(barrier, devices - 1)

    def kv_copy(k):
        to = lax.rem(me + k, devices)
        return remote(kv_send.at[to], kv_recv.at[me], kv_ssem.at[k], kv_rsem.at[k], to)

    def kv_go(k, carry):
        kv_copy(k).start()
        return carry

    lax.fori_loop(1, devices, kv_go, 0)

    for copy in loads[1:]:
        copy.wait()

    def per_seq(values, shape):
        at = lax.broadcasted_iota(jnp.int32, shape, 0)
        return sum(jnp.where(at == s, v, 0) for s, v in enumerate(values))

    tokens = kv_ref.shape[0] * PAGE_TOKENS
    limit = per_seq([blocks[s] for s in range(seqs)], (seqs, tokens))
    page_of = lax.broadcasted_iota(jnp.int32, (seqs, tokens), 1) // PAGE_TOKENS
    held = jnp.zeros((seqs, tokens), f32)
    for b in range(table_ref.shape[1]):
        hit = (page_of == table_ref[:, b : b + 1]) & (limit > b)
        held = held + jnp.where(hit, 1.0, 0.0)
    held = jnp.concatenate([held] * group, 0)

    def heads(h):
        rows = q_ref[...].astype(f32)
        return jnp.concatenate(
            [
                rows[:, (h * group + g) * HEAD_SIZE : (h * group + g + 1) * HEAD_SIZE]
                for g in range(group)
            ],
            0,
        )

    def own(h, at):
        both = dkv_ref[...].astype(f32)
        return jnp.concatenate(
            [both[:, at, h * HEAD_SIZE : (h + 1) * HEAD_SIZE]] * group, 0
        )

    def weigh(scores, times, own_score):
        scores = jnp.where(times > 0, scores, masked_score)
        peak = jnp.maximum(jnp.max(scores, -1, keepdims=True), own_score)
        weight = times * jnp.exp(scores - peak)
        own_weight = jnp.exp(own_score - peak)
        total = jnp.sum(weight, -1, keepdims=True) + own_weight
        return (weight / total).astype(bf16), (own_weight / total).astype(bf16).astype(f32)

    def dot_t(a, b):
        return lax.dot_general(a, b, (((1,), (1,)), ((), ())), preferred_element_type=f32)

    def spread(h, mixed, old):
        for g in range(group):
            at = slice((h * group + g) * HEAD_SIZE, (h * group + g + 1) * HEAD_SIZE)
            rows = mixed[g * seqs : (g + 1) * seqs]
            if old:
                attn[:, at] = rows
            else:
                attn[:, at] = jnp.where(is_new, rows, attn[:, at])

    own_scores = []
    for h in range(KEY_VALUE_HEADS):
        at = slice(h * HEAD_SIZE, (h + 1) * HEAD_SIZE)
        queries = heads(h)
        own_score = jnp.sum(queries * own(h, 0), -1, keepdims=True) * scale
        own_scores.append(own_score)
        keys = kv_ref[:, 0, :, at].reshape(tokens, HEAD_SIZE)
        values = kv_ref[:, 1, :, at].reshape(tokens, HEAD_SIZE)
        probs, own_prob = weigh(dot_t(queries.astype(bf16), keys) * scale, held, own_score)
        mixed = jnp.dot(probs, values, preferred_element_type=f32) + own_prob * own(h, 1)
        spread(h, mixed, True)

    def kv_end(k, carry):
        kv_copy(k).wait()
        return carry

    lax.fori_loop(1, devices, kv_end, 0)

    fresh = devices * PAGE_TOKENS
    slot = lax.rem(lax.broadcasted_iota(jnp.int32, (seqs * group, 1), 0), seqs)
    length = per_seq([prompt_lengths[p] for p in own_picks], (seqs, fresh))
    ahead = lax.broadcasted_iota(jnp.int32, (seqs, fresh), 1) // PAGE_TOKENS < length
    is_new = lax.broadcasted_iota(jnp.int32, (seqs, HEAD_SIZE), 0) < new_count
    allowed = jnp.concatenate([jnp.where(ahead, 1.0, 0.0)] * group, 0)
    for h in range(KEY_VALUE_HEADS):
        at = slice(h * HEAD_SIZE, (h + 1) * HEAD_SIZE)
        queries = heads(h).astype(bf16)
        scores = jnp.zeros((seqs * group, fresh), f32)
        for r in range(MAXP):
            keys = kv_recv[:, r, 0, :, at].reshape(fresh, HEAD_SIZE)
            scores = jnp.where(slot == r, dot_t(queries, keys), scores)
        probs, own_prob = weigh(scores * scale, allowed, own_scores[h])
        mixed = jnp.zeros((seqs * group, HEAD_SIZE), f32)
        for r in range(MAXP):
            values = kv_recv[:, r, 1, :, at].reshape(fresh, HEAD_SIZE)
            mixed = jnp.where(
                slot == r, jnp.dot(probs, values, preferred_element_type=f32), mixed
            )
        spread(h, mixed + own_prob * own(h, 1), False)

    attention = attn[...].astype(bf16).astype(f32)
    wide = (hidden_ref[...].astype(f32) + attention).astype(bf16).astype(f32)
    attn[...] = wide
    mean = jnp.mean(wide * wide, -1, keepdims=True)
    normed = (wide * lax.rsqrt(mean + norm_eps) * gain_ref[...]).astype(bf16)
    mine = place(line, row, core)
    x_all[mine] = normed

    other_row = device(line, 1 - row, core)
    other_core = device(line, row, 1 - core)

    def pass_on(pool, spot, at, to):
        buffer, cols, n, ssem, rsem = pool
        ref = buffer.at[spot, :, cols]
        return remote(ref, ref, ssem.at[n, at], rsem.at[n, spot], to)

    def first_hops(pool):
        copies = [pass_on(pool, mine, 0, other_row)]
        for k in range(1, lines):
            copies.append(pass_on(pool, mine, k, device(lax.rem(line + k, lines), row, core)))
        copies.append(pass_on(pool, mine, lines, other_core))
        for copy in copies:
            copy.start()
        return copies

    def arrived(pool, spot):
        pass_on(pool, spot, 0, other_core).wait_recv()

    pieces = x_rsem.shape[0] - 1
    piece = D // pieces
    pools = [
        (x_all, slice(n * piece, (n + 1) * piece), n, x_ssem, x_rsem) for n in range(pieces)
    ]
    sent = []
    for pool in pools:
        sent += first_hops(pool)

    logits = dot_t(normed, router_ref[...])
    experts = logits.shape[1]
    expert_of = lax.broadcasted_iota(jnp.int32, (seqs, experts), 1)
    times = jnp.zeros((seqs, experts), f32)
    for k in range(ids_ref.shape[1]):
        times = times + jnp.where(ids_ref[:, k : k + 1] == expert_of, 1.0, 0.0)
    picked = jnp.where(times > 0, logits, masked_score)
    gate = times * jnp.exp(picked - jnp.max(picked, -1, keepdims=True))
    gate = gate / jnp.sum(gate, -1, keepdims=True)
    gates[mine] = jnp.concatenate([gate] * (128 // experts), 1)
    pools.append((gates, slice(0, 128), pieces, x_ssem, x_rsem))
    sent += first_hops(pools[-1])

    def over_core(k):
        spot = place(lax.rem(line + k, lines), 1 - row, core)
        for pool in pools:
            arrived(pool, spot)
            copy = pass_on(pool, spot, 3 * lines - 1 + k, other_core)
            copy.start()
            sent.append(copy)

    over_core(0)
    for k in range(1, lines):
        spot = place(lax.rem(line + k, lines), row, core)
        for pool in pools:
            arrived(pool, spot)
            for step, to in ((0, other_row), (1, other_core)):
                copy = pass_on(pool, spot, lines + 2 * k - 1 + step, to)
                copy.start()
                sent.append(copy)
    for k in range(1, lines):
        over_core(k)
    for at_row in range(2):
        for k in range(lines):
            for pool in pools:
                arrived(pool, place(k, at_row, 1 - core))

    weights[0].wait()
    weights[1].wait()
    total = devices * seqs
    hidden = w_gate.shape[1]
    step = min(512, D)

    def project(i, carry):
        at = pl.ds(pl.multiple_of(i * step, step), step)
        x = x_all[:, :, at].reshape(total, step)
        return (
            carry[0] + jnp.dot(x, w_gate[at, :], preferred_element_type=f32),
            carry[1] + jnp.dot(x, w_up[at, :], preferred_element_type=f32),
        )

    zeros = jnp.zeros((total, hidden), f32)
    gate_proj, up_proj = lax.fori_loop(0, D // step, project, (zeros, zeros))
    lanes = lax.broadcasted_iota(jnp.int32, (total, 128), 1)
    scaled = jnp.sum(
        jnp.where(lanes == me // 2, gates[...].reshape(total, 128), 0.0), -1, keepdims=True
    )
    activated = (gate_proj / (1.0 + jnp.exp(-gate_proj)) * up_proj * scaled).astype(bf16)

    weights[2].wait()
    chunks = c_sem.shape[1]
    width = D // chunks

    def cut(i):
        return slice(i * width, (i + 1) * width)

    def core_copy(i):
        return remote(
            part.at[1 - core, :, :, :, cut(i)],
            core_recv.at[:, :, :, cut(i)],
            c_sem.at[0, i],
            c_sem.at[1, i],
            other_core,
        )

    def row_copy(i):
        return remote(
            y_send.at[:, :, cut(i)],
            y_recv.at[:, :, cut(i)],
            y_sem.at[0, i],
            y_sem.at[1, i],
            other_row,
        )

    def line_copy(i, k):
        to = lax.rem(line + k, lines)
        return remote(
            z_send.at[k, :, cut(i)],
            z_recv.at[k, :, cut(i)],
            zs_sem.at[k, i],
            zr_sem.at[k, i],
            device(to, row, core),
        )

    for i in range(chunks):
        rows = jnp.dot(activated, w_down[:, cut(i)], preferred_element_type=f32)
        part[:, :, :, :, cut(i)] = rows.astype(bf16).reshape(2, 2, lines, seqs, width)
        core_copy(i).start()
    for i in range(chunks):
        core_copy(i).wait()
        y_send[:, :, cut(i)] = (
            part[core, 1 - row, :, :, cut(i)].astype(f32)
            + core_recv[1 - row, :, :, cut(i)].astype(f32)
        ).astype(bf16)
        row_copy(i).start()
    for i in range(chunks):
        row_copy(i).wait()

        def summed(at_line):
            return (
                part[core, row, at_line, :, cut(i)].astype(f32)
                + core_recv[row, at_line, :, cut(i)].astype(f32)
                + y_recv[at_line, :, cut(i)].astype(f32)
            )

        for k in range(1, lines):
            z_send[k, :, cut(i)] = summed(lax.rem(line + k, lines)).astype(bf16)
            line_copy(i, k).start()
        kept[:, cut(i)] = attn[:, cut(i)] + summed(line)
    for i in range(chunks):
        answer = kept[:, cut(i)]
        for k in range(1, lines):
            line_copy(i, k).wait()
            answer = answer + z_recv[k, :, cut(i)].astype(f32)
        out_ref[:, cut(i)] = answer.astype(bf16)
    for copy in sent:
        copy.wait_send()


def dense(
    hidden_in,
    queries,
    decode_key_value,
    local_kv,
    page_table,
    seq_blocks,
    prompt_kv,
    prompt_owner,
    prompt_pages,
    norm_gain,
    router,
    w_gate,
    w_up,
    w_down,
    route_ids,
):
    devices = lax.axis_size("expert")
    seqs = hidden_in.shape[0]
    hidden = w_gate.shape[2]
    lines = devices // 4
    bf16, f32 = jnp.bfloat16, jnp.float32
    chunks = 8
    pieces = 2
    loaded = (
        prompt_kv[0],
        queries,
        decode_key_value,
        page_table,
        local_kv,
        hidden_in,
        norm_gain[None, :],
        router.T,
        route_ids,
    )
    smem = pl.BlockSpec(memory_space=pltpu.SMEM)
    vmem = pl.BlockSpec(memory_space=pltpu.VMEM)
    hbm = pl.BlockSpec(memory_space=pltpu.HBM)
    dma = pltpu.SemaphoreType.DMA
    page = (MAXP, 2, PAGE_TOKENS, KEY_VALUE_HEADS * HEAD_SIZE)
    return pl.pallas_call(
        functools.partial(layer_kernel, devices),
        out_shape=jax.ShapeDtypeStruct((seqs, D), bf16),
        in_specs=[smem] * 3 + [hbm] * (len(loaded) + 3),
        out_specs=vmem,
        scratch_shapes=[pltpu.VMEM(a.shape, a.dtype) for a in loaded]
        + [
            pltpu.VMEM((D, hidden), bf16),
            pltpu.VMEM((D, hidden), bf16),
            pltpu.VMEM((hidden, D), bf16),
            pltpu.VMEM((devices,) + page, bf16),
            pltpu.VMEM((devices,) + page, bf16),
            pltpu.VMEM((seqs, D), f32),
            pltpu.VMEM((devices, seqs, D), bf16),
            pltpu.VMEM((devices, seqs, 128), f32),
            pltpu.VMEM((2, 2, lines, seqs, D), bf16),
            pltpu.VMEM((2, lines, seqs, D), bf16),
            pltpu.VMEM((lines, seqs, D), bf16),
            pltpu.VMEM((lines, seqs, D), bf16),
            pltpu.VMEM((lines, seqs, D), bf16),
            pltpu.VMEM((lines, seqs, D), bf16),
            pltpu.VMEM((seqs, D), f32),
            dma((len(loaded),)),
            dma((3,)),
            dma((devices,)),
            dma((devices,)),
            dma((pieces + 1, 4 * lines)),
            dma((pieces + 1, devices)),
            dma((2, chunks)),
            dma((2, chunks)),
            dma((lines, chunks)),
            dma((lines, chunks)),
        ],
        compiler_params=pltpu.CompilerParams(
            collective_id=0, has_side_effects=True, vmem_limit_bytes=67043328
        ),
    )(prompt_owner, prompt_pages, seq_blocks, *loaded, w_gate, w_up, w_down)


def local(*arrays):
    devices = lax.axis_size("expert")
    experts = arrays[10].shape[1]
    if experts == TOPK and devices == 2 * experts and devices % 4 == 0:
        return dense(*arrays)
    return routed(*arrays)


def solution(mesh):
    return jax.shard_map(
        local,
        mesh=mesh,
        in_specs=(
            P(("groups", "expert"), None),
            P(("groups", "expert"), None),
            P(("groups", "expert"), None, None),
            P(("groups", "expert"), None, None, None),
            P(("groups", "expert"), None),
            P(("groups", "expert")),
            P(("groups", "expert"), None, None, None, None),
            P("groups"),
            P("groups"),
            P(),
            P(),
            P("expert", None, None),
            P("expert", None, None),
            P("expert", None, None),
            P(("groups", "expert"), None),
        ),
        out_specs=P(("groups", "expert"), None),
        check_vma=False,
    )
```

profile of v0, /device:TPU:0, one launch (start us, length us, event | category | flops | bytes accessed | tf_op | source)
XLA Modules:
  0.0 52.5 jit_solution(8223473205942497928)
XLA Ops:
  0.0 51.0 %shard_map.145 = bf16[8,4096]{1,0:T(8,128)(2,1)} custom-call(s32[16]{0:T(128)} %owners.1, s32[16]{0:T(128)} %prompt_lengths.1, s32[8]{0:T(128)} %blocks.1, bf16[16,2,16,256]{3,2,1,0:T(8,128)(2,1)} %bitcast.3, bf16[8,4096]{1,0:T(8,128)(2,1)} %q_hbm.1, bf16[8,2,256]{2,1,0:T(2,128)(2,1)} %dkv_hbm.1, s32[8,16]{1,0:T(8,128)} %table_hbm.1, ...), custom_call_target="tpu_custom_call" | custom-call | tf_op jit(solution)/shard_map/pallas_call | solution.py:636
  51.1 1.5 %copy.17 = bf16[8,4096]{1,0:T(8,128)(2,1)} copy(bf16[8,4096]{1,0:T(8,128)(2,1)} %shard_map.145) | data formatting | bytes 131072
where the time goes:
time: 52.7 us; the launch traced here: 52.5 us
  Pallas kernels  51 us (97%)
  local copies, waits for them, and re-layouts  1.47 us (3%)
    pallas_call x1, Pallas kernels, dense(): pl.pallas_call(functools.partial(layer_kernel, devices), out_shape=jax.Sh...  51 us
    unnamed x1, local copies, waits for them, and re-layouts  1.47 us

commit v1 on v0

--- a/solution.py
+++ b/solution.py
@@ -204,7 +204,7 @@
     gate_hbm,
     up_hbm,
     down_hbm,
-    out_ref,
+    out_hbm,
     pages_ref,
     q_ref,
     dkv_ref,
@@ -214,42 +214,67 @@
     gain_ref,
     router_ref,
     ids_ref,
-    w_gate,
-    w_up,
+    w_in,
     w_down,
-    kv_send,
-    kv_recv,
+    other_pages,
+    q_send,
+    q_recv,
+    o_send,
+    o_recv,
+    lse_send,
+    lse_recv,
     attn,
-    x_all,
-    gates,
-    part,
-    core_recv,
+    x_a,
+    gates_a,
+    x_b,
+    gates_b,
+    part_a,
+    core_a,
     y_send,
     y_recv,
     z_send,
     z_recv,
     kept,
+    part_b,
+    core_b,
+    sum_b,
+    recv_b,
+    out_ref,
     in_sem,
     w_sem,
-    kv_ssem,
-    kv_rsem,
-    x_ssem,
-    x_rsem,
+    page_sem,
+    q_sem,
+    o_sem,
+    lse_sem,
+    xa_ssem,
+    xa_rsem,
+    xb_sem,
+    xf_sem,
     c_sem,
     y_sem,
     zs_sem,
     zr_sem,
+    cb_sem,
+    rb_sem,
+    out_sem,
 ):
     f32, bf16 = jnp.float32, jnp.bfloat16
     me = lax.axis_index("expert")
     lines = devices // 4
+    chips = devices // 2
     core, row, line = lax.rem(me, 2), lax.rem(me // 2, 2), me // 4
+    unit = row * lines + line
     seqs = hidden_ref.shape[0]
     group = QUERY_HEADS // KEY_VALUE_HEADS
     scale = 1.0 / math.sqrt(HEAD_SIZE)
+    old_rows = pl.ds(MAXP, seqs - MAXP)
+    new_rows = pl.ds(0, MAXP)
 
     def device(at_line, at_row, at_core):
         return (at_line * 2 + at_row) * 2 + at_core
+
+    def device_of(at_unit, at_core):
+        return device(lax.rem(at_unit, lines), at_unit // lines, at_core)
 
     def place(at_line, at_row, at_core):
         return (at_core * 2 + at_row) * lines + at_line
@@ -264,12 +289,16 @@
             device_id_type=pl.DeviceIdType.MESH,
         )
 
+    other_row = device(line, 1 - row, core)
+    other_core = device(line, row, 1 - core)
+    mine = place(line, row, core)
+
     loads = [
         pltpu.make_async_copy(a, b, in_sem.at[i])
         for i, (a, b) in enumerate(
             (
+                (q_hbm, q_ref),
                 (pages_hbm, pages_ref),
-                (q_hbm, q_ref),
                 (dkv_hbm, dkv_ref),
                 (table_hbm, table_ref),
                 (kv_hbm, kv_ref),
@@ -280,13 +309,12 @@
             )
         )
     ]
+    hidden = w_down.shape[0]
     weights = [
-        pltpu.make_async_copy(a.at[0], b, w_sem.at[i])
-        for i, (a, b) in enumerate(((gate_hbm, w_gate), (up_hbm, w_up), (down_hbm, w_down)))
+        pltpu.make_async_copy(gate_hbm.at[0], w_in.at[:, pl.ds(0, hidden)], w_sem.at[0]),
+        pltpu.make_async_copy(up_hbm.at[0], w_in.at[:, pl.ds(hidden, hidden)], w_sem.at[1]),
+        pltpu.make_async_copy(down_hbm.at[0], w_down, w_sem.at[2]),
     ]
-    for copy in loads + weights:
-        copy.start()
-
     barrier = pltpu.get_barrier_semaphore()
 
     def greet(k, carry):
@@ -299,43 +327,62 @@
         return carry
 
     lax.fori_loop(1, devices, greet, 0)
-
-    prompts = owners.shape[0]
-
-    def named(o):
-        first, last, number = jnp.int32(0), jnp.int32(0), jnp.int32(0)
-        for p in range(prompts):
-            hit = owners[p] == o
-            last = jnp.where(hit, p, last)
-            number = number + hit.astype(jnp.int32)
-        for p in reversed(range(prompts)):
-            first = jnp.where(owners[p] == o, p, first)
-        return (first, last), number
-
-    def stage(o, carry):
-        picks, _ = named(o)
-        for r in range(MAXP):
-            kv_send[o, r] = pages_ref[picks[r]]
+    for copy in loads + weights:
+        copy.start()
+
+    fold = seqs // MAXP
+    lane_heads = QUERY_HEADS // fold
+    packed = lane_heads * HEAD_SIZE
+    per_kv = lane_heads // KEY_VALUE_HEADS
+    sub = lax.broadcasted_iota(jnp.int32, (seqs, packed), 0) // MAXP
+
+    def head_cols(h):
+        return slice(h * HEAD_SIZE, (h + 1) * HEAD_SIZE)
+
+    def turn(x, by):
+        by = by % seqs
+        return x if by == 0 else pltpu.roll(x, by, 0)
+
+    def pack(rows):
+        out = None
+        for f in range(fold):
+            wide = turn(
+                jnp.concatenate([rows[:, head_cols(fold * hh + f)] for hh in range(lane_heads)], 1),
+                MAXP * f,
+            )
+            out = wide if f == 0 else jnp.where(sub == f, wide, out)
+        return out
+
+    def spread_rows(rows):
+        out = rows
+        at = lax.broadcasted_iota(jnp.int32, rows.shape, 0) // MAXP
+        for f in range(1, fold):
+            out = jnp.where(at == f, turn(rows, MAXP * f), out)
+        return out
+
+    def dot_t(a, b):
+        return lax.dot_general(a, b, (((1,), (1,)), ((), ())), preferred_element_type=f32)
+
+    loads[0].wait()
+    q_packed = pack(q_ref[...].astype(f32))
+    q_send[...] = q_packed.astype(bf16)
+    pl.semaphore_wait(barrier, devices - 1)
+
+    def q_copy(k):
+        to = device_of(lax.rem(unit + k, chips), core)
+        return remote(q_send, q_recv.at[unit], q_sem.at[0, k], q_sem.at[1, k], to)
+
+    def q_go(k, carry):
+        q_copy(k).start()
         return carry
 
-    loads[0].wait()
-    lax.fori_loop(0, devices, stage, 0)
-    own_picks, new_count = named(me)
-    for r in range(MAXP):
-        kv_recv[me, r] = pages_ref[own_picks[r]]
-    pl.semaphore_wait(barrier, devices - 1)
-
-    def kv_copy(k):
-        to = lax.rem(me + k, devices)
-        return remote(kv_send.at[to], kv_recv.at[me], kv_ssem.at[k], kv_rsem.at[k], to)
-
-    def kv_go(k, carry):
-        kv_copy(k).start()
-        return carry
-
-    lax.fori_loop(1, devices, kv_go, 0)
-
-    for copy in loads[1:]:
+    lax.fori_loop(1, chips, q_go, 0)
+    q_recv[unit] = q_packed.astype(bf16)
+    loads[1].wait()
+    page_copy = remote(pages_ref, other_pages, page_sem.at[0], page_sem.at[1], other_core)
+    page_copy.start()
+
+    for copy in loads[2:]:
         copy.wait()
 
     def per_seq(values, shape):
@@ -353,19 +400,11 @@
 
     def heads(h):
         rows = q_ref[...].astype(f32)
-        return jnp.concatenate(
-            [
-                rows[:, (h * group + g) * HEAD_SIZE : (h * group + g + 1) * HEAD_SIZE]
-                for g in range(group)
-            ],
-            0,
-        )
+        return jnp.concatenate([rows[:, head_cols(h * group + g)] for g in range(group)], 0)
 
     def own(h, at):
         both = dkv_ref[...].astype(f32)
-        return jnp.concatenate(
-            [both[:, at, h * HEAD_SIZE : (h + 1) * HEAD_SIZE]] * group, 0
-        )
+        return jnp.concatenate([both[:, at, head_cols(h)]] * group, 0)
 
     def weigh(scores, times, own_score):
         scores = jnp.where(times > 0, scores, masked_score)
@@ -375,78 +414,50 @@
         total = jnp.sum(weight, -1, keepdims=True) + own_weight
         return (weight / total).astype(bf16), (own_weight / total).astype(bf16).astype(f32)
 
-    def dot_t(a, b):
-        return lax.dot_general(a, b, (((1,), (1,)), ((), ())), preferred_element_type=f32)
-
-    def spread(h, mixed, old):
-        for g in range(group):
-            at = slice((h * group + g) * HEAD_SIZE, (h * group + g + 1) * HEAD_SIZE)
-            rows = mixed[g * seqs : (g + 1) * seqs]
-            if old:
-                attn[:, at] = rows
-            else:
-                attn[:, at] = jnp.where(is_new, rows, attn[:, at])
-
-    own_scores = []
     for h in range(KEY_VALUE_HEADS):
-        at = slice(h * HEAD_SIZE, (h + 1) * HEAD_SIZE)
+        at = head_cols(h)
         queries = heads(h)
         own_score = jnp.sum(queries * own(h, 0), -1, keepdims=True) * scale
-        own_scores.append(own_score)
         keys = kv_ref[:, 0, :, at].reshape(tokens, HEAD_SIZE)
         values = kv_ref[:, 1, :, at].reshape(tokens, HEAD_SIZE)
         probs, own_prob = weigh(dot_t(queries.astype(bf16), keys) * scale, held, own_score)
         mixed = jnp.dot(probs, values, preferred_element_type=f32) + own_prob * own(h, 1)
-        spread(h, mixed, True)
-
-    def kv_end(k, carry):
-        kv_copy(k).wait()
-        return carry
-
-    lax.fori_loop(1, devices, kv_end, 0)
-
-    fresh = devices * PAGE_TOKENS
-    slot = lax.rem(lax.broadcasted_iota(jnp.int32, (seqs * group, 1), 0), seqs)
-    length = per_seq([prompt_lengths[p] for p in own_picks], (seqs, fresh))
-    ahead = lax.broadcasted_iota(jnp.int32, (seqs, fresh), 1) // PAGE_TOKENS < length
-    is_new = lax.broadcasted_iota(jnp.int32, (seqs, HEAD_SIZE), 0) < new_count
-    allowed = jnp.concatenate([jnp.where(ahead, 1.0, 0.0)] * group, 0)
-    for h in range(KEY_VALUE_HEADS):
-        at = slice(h * HEAD_SIZE, (h + 1) * HEAD_SIZE)
-        queries = heads(h).astype(bf16)
-        scores = jnp.zeros((seqs * group, fresh), f32)
-        for r in range(MAXP):
-            keys = kv_recv[:, r, 0, :, at].reshape(fresh, HEAD_SIZE)
-            scores = jnp.where(slot == r, dot_t(queries, keys), scores)
-        probs, own_prob = weigh(scores * scale, allowed, own_scores[h])
-        mixed = jnp.zeros((seqs * group, HEAD_SIZE), f32)
-        for r in range(MAXP):
-            values = kv_recv[:, r, 1, :, at].reshape(fresh, HEAD_SIZE)
-            mixed = jnp.where(
-                slot == r, jnp.dot(probs, values, preferred_element_type=f32), mixed
-            )
-        spread(h, mixed + own_prob * own(h, 1), False)
-
-    attention = attn[...].astype(bf16).astype(f32)
-    wide = (hidden_ref[...].astype(f32) + attention).astype(bf16).astype(f32)
-    attn[...] = wide
-    mean = jnp.mean(wide * wide, -1, keepdims=True)
-    normed = (wide * lax.rsqrt(mean + norm_eps) * gain_ref[...]).astype(bf16)
-    mine = place(line, row, core)
-    x_all[mine] = normed
-
-    other_row = device(line, 1 - row, core)
-    other_core = device(line, row, 1 - core)
+        for g in range(group):
+            attn[:, head_cols(h * group + g)] = mixed[g * seqs : (g + 1) * seqs]
+
+    def residual_of(attention):
+        rounded = attention.astype(bf16).astype(f32)
+        return (hidden_ref[...].astype(f32) + rounded).astype(bf16).astype(f32)
+
+    def norm_of(wide):
+        mean = jnp.mean(wide * wide, -1, keepdims=True)
+        return (wide * lax.rsqrt(mean + norm_eps) * gain_ref[...]).astype(bf16)
+
+    def gate_of(normed):
+        logits = dot_t(normed, router_ref[...])
+        experts = logits.shape[1]
+        expert_of = lax.broadcasted_iota(jnp.int32, (seqs, experts), 1)
+        times = jnp.zeros((seqs, experts), f32)
+        for k in range(ids_ref.shape[1]):
+            times = times + jnp.where(ids_ref[:, k : k + 1] == expert_of, 1.0, 0.0)
+        picked = jnp.where(times > 0, logits, masked_score)
+        gate = times * jnp.exp(picked - jnp.max(picked, -1, keepdims=True))
+        gate = gate / jnp.sum(gate, -1, keepdims=True)
+        return jnp.concatenate([gate] * (128 // experts), 1)
+
+    normed = norm_of(residual_of(attn[...]))
+    x_a[mine] = normed
 
     def pass_on(pool, spot, at, to):
-        buffer, cols, n, ssem, rsem = pool
-        ref = buffer.at[spot, :, cols]
-        return remote(ref, ref, ssem.at[n, at], rsem.at[n, spot], to)
+        buffer, rows, n = pool
+        ref = buffer.at[spot, rows]
+        return remote(ref, ref, xa_ssem.at[n, at], xa_rsem.at[n, spot], to)
 
     def first_hops(pool):
-        copies = [pass_on(pool, mine, 0, other_row)]
+        copies = []
         for k in range(1, lines):
             copies.append(pass_on(pool, mine, k, device(lax.rem(line + k, lines), row, core)))
+        copies.append(pass_on(pool, mine, 0, other_row))
         copies.append(pass_on(pool, mine, lines, other_core))
         for copy in copies:
             copy.start()
@@ -455,27 +466,87 @@
     def arrived(pool, spot):
         pass_on(pool, spot, 0, other_core).wait_recv()
 
-    pieces = x_rsem.shape[0] - 1
-    piece = D // pieces
-    pools = [
-        (x_all, slice(n * piece, (n + 1) * piece), n, x_ssem, x_rsem) for n in range(pieces)
-    ]
-    sent = []
-    for pool in pools:
-        sent += first_hops(pool)
-
-    logits = dot_t(normed, router_ref[...])
-    experts = logits.shape[1]
-    expert_of = lax.broadcasted_iota(jnp.int32, (seqs, experts), 1)
-    times = jnp.zeros((seqs, experts), f32)
-    for k in range(ids_ref.shape[1]):
-        times = times + jnp.where(ids_ref[:, k : k + 1] == expert_of, 1.0, 0.0)
-    picked = jnp.where(times > 0, logits, masked_score)
-    gate = times * jnp.exp(picked - jnp.max(picked, -1, keepdims=True))
-    gate = gate / jnp.sum(gate, -1, keepdims=True)
-    gates[mine] = jnp.concatenate([gate] * (128 // experts), 1)
-    pools.append((gates, slice(0, 128), pieces, x_ssem, x_rsem))
-    sent += first_hops(pools[-1])
+    pools = [(x_a, old_rows, 0), (gates_a, pl.ds(0, seqs), 1)]
+    sent = first_hops(pools[0])
+    gates_a[mine] = gate_of(normed)
+    sent += first_hops(pools[1])
+
+    prompts = owners.shape[0]
+    shape = (1, prompts * PAGE_TOKENS)
+    prompt_of = lax.broadcasted_iota(jnp.int32, shape, 1) // PAGE_TOKENS
+    owner_of, length_of = jnp.zeros(shape, jnp.int32), jnp.zeros(shape, jnp.int32)
+    for p in range(prompts):
+        owner_of = jnp.where(prompt_of == p, owners[p], owner_of)
+        length_of = jnp.where(prompt_of == p, prompt_lengths[p], length_of)
+    rank_of = jnp.zeros(shape, jnp.int32)
+    for p in range(prompts):
+        rank_of = rank_of + jnp.where((owner_of == owners[p]) & (prompt_of > p), 1, 0)
+    slots = chips * seqs
+    at_row = lax.broadcasted_iota(jnp.int32, (slots, 1), 0)
+    row_unit = at_row // seqs
+    row_owner = device_of(row_unit, core)
+    match = (owner_of == row_owner) & (rank_of == lax.rem(at_row, MAXP))
+
+    def allowed_at(position):
+        ok = match & (length_of > position)
+        return jnp.concatenate([jnp.where(ok, 1.0, 0.0)] * per_kv, 0)
+
+    allowed = (allowed_at(me), allowed_at(other_core))
+    page_copy.wait_recv()
+
+    def q_end(k, carry):
+        q_copy(k).wait_recv()
+        return carry
+
+    lax.fori_loop(1, chips, q_end, 0)
+    lane_of = lax.broadcasted_iota(jnp.int32, (slots, 128), 1)
+    lse_all = jnp.zeros((slots, 128), f32)
+    for h in range(KEY_VALUE_HEADS):
+        at = head_cols(h)
+        lanes = [h * per_kv + j for j in range(per_kv)]
+        queries = jnp.concatenate(
+            [q_recv[:, :, head_cols(hh)].reshape(slots, HEAD_SIZE) for hh in lanes], 0
+        )
+        scores = []
+        for ref, ok in zip((pages_ref, other_pages), allowed):
+            keys = ref[:, 0, :, at].reshape(prompts * PAGE_TOKENS, HEAD_SIZE)
+            scores.append(jnp.where(ok > 0, dot_t(queries, keys) * scale, masked_score))
+        peak = jnp.maximum(
+            jnp.max(scores[0], -1, keepdims=True), jnp.max(scores[1], -1, keepdims=True)
+        )
+        total = jnp.zeros((slots * per_kv, 1), f32)
+        mixed = jnp.zeros((slots * per_kv, HEAD_SIZE), f32)
+        for ref, ok, score in zip((pages_ref, other_pages), allowed, scores):
+            weight = ok * jnp.exp(score - peak)
+            total = total + jnp.sum(weight, -1, keepdims=True)
+            values = ref[:, 1, :, at].reshape(prompts * PAGE_TOKENS, HEAD_SIZE)
+            mixed = mixed + jnp.dot(weight.astype(bf16), values, preferred_element_type=f32)
+        some = total > 0
+        safe = jnp.where(some, total, 1.0)
+        mixed = mixed / safe
+        lse = jnp.where(some, peak + jnp.log(safe), masked_score)
+        for j, hh in enumerate(lanes):
+            rows = slice(j * slots, (j + 1) * slots)
+            o_send[:, :, head_cols(hh)] = mixed[rows].astype(bf16).reshape(chips, seqs, HEAD_SIZE)
+            lse_all = jnp.where(lane_of == hh, lse[rows], lse_all)
+    lse_send[...] = lse_all.reshape(chips, seqs, 128)
+
+    def o_copy(k):
+        to = lax.rem(unit + k, chips)
+        at = device_of(to, core)
+        return (
+            remote(o_send.at[to], o_recv.at[unit], o_sem.at[0, k], o_sem.at[1, k], at),
+            remote(lse_send.at[to], lse_recv.at[unit], lse_sem.at[0, k], lse_sem.at[1, k], at),
+        )
+
+    def o_go(k, carry):
+        for copy in o_copy(k):
+            copy.start()
+        return carry
+
+    lax.fori_loop(1, chips, o_go, 0)
+    o_recv[unit] = o_send[unit]
+    lse_recv[unit] = lse_send[unit]
 
     def over_core(k):
         spot = place(lax.rem(line + k, lines), 1 - row, core)
@@ -494,36 +565,98 @@
                 copy = pass_on(pool, spot, lines + 2 * k - 1 + step, to)
                 copy.start()
                 sent.append(copy)
+
+    own_both = dkv_ref[...].astype(f32)
+    own_key = spread_rows(own_both[:, 0])
+    own_value = spread_rows(own_both[:, 1])
+    lane = lax.broadcasted_iota(jnp.int32, (seqs, 128), 1)
+    own_score = jnp.zeros((seqs, 128), f32)
+    for hh in range(lane_heads):
+        score = jnp.sum(
+            q_packed[:, head_cols(hh)] * own_key[:, head_cols(hh // per_kv)], -1, keepdims=True
+        )
+        own_score = jnp.where(lane == hh, score * scale, own_score)
+    new_count = jnp.int32(0)
+    for p in range(prompts):
+        new_count = new_count + (owners[p] == me).astype(jnp.int32)
+    is_new = lax.broadcasted_iota(jnp.int32, (seqs, HEAD_SIZE), 0) < new_count
+
+    def o_end(k, carry):
+        for copy in o_copy(k):
+            copy.wait_recv()
+        return carry
+
+    lax.fori_loop(1, chips, o_end, 0)
+    peak = own_score
+    for u in range(chips):
+        peak = jnp.maximum(peak, lse_recv[u])
+    shares = [jnp.exp(lse_recv[u] - peak) for u in range(chips)]
+    own_share = jnp.exp(own_score - peak)
+    total = own_share
+    for share in shares:
+        total = total + share
+    inverse = 1.0 / total
+    shares = [share * inverse for share in shares]
+    own_share = own_share * inverse
+    for hh in range(lane_heads):
+        at = head_cols(hh)
+        mixed = own_share[:, hh : hh + 1] * own_value[:, head_cols(hh // per_kv)]
+        for u in range(chips):
+            mixed = mixed + shares[u][:, hh : hh + 1] * o_recv[u, :, at].astype(f32)
+        for f in range(fold):
+            cols = head_cols(fold * hh + f)
+            attn[:, cols] = jnp.where(is_new, turn(mixed, -MAXP * f), attn[:, cols])
+    wide = residual_of(attn[...])
+    attn[...] = wide
+    normed = norm_of(wide)
+    x_b[mine] = normed
+
+    b_pools = [(x_b, new_rows, 0), (gates_b, pl.ds(0, seqs), 1)]
+
+    def b_copy(pool, k):
+        buffer, rows, n = pool
+        ref = buffer.at[mine, rows]
+        to = device_of(lax.rem(unit + k, chips), core)
+        return remote(ref, ref, xb_sem.at[0, n, k], xb_sem.at[1, n, k], to)
+
+    def b_forward(pool, k):
+        buffer, rows, n = pool
+        ref = buffer.at[core * chips + lax.rem(unit + chips - k, chips), rows]
+        return remote(ref, ref, xf_sem.at[0, n, k], xf_sem.at[1, n, k], other_core)
+
+    def b_first(pool):
+        def go(k, carry):
+            b_copy(pool, k).start()
+            return carry
+
+        lax.fori_loop(1, chips, go, 0)
+        b_forward(pool, 0).start()
+
+    b_first(b_pools[0])
+    gates_b[mine] = gate_of(normed)
+    b_first(b_pools[1])
+
     for k in range(1, lines):
         over_core(k)
     for at_row in range(2):
         for k in range(lines):
             for pool in pools:
                 arrived(pool, place(k, at_row, 1 - core))
-
-    weights[0].wait()
-    weights[1].wait()
+    for copy in weights:
+        copy.wait()
     total = devices * seqs
-    hidden = w_gate.shape[1]
-    step = min(512, D)
-
-    def project(i, carry):
-        at = pl.ds(pl.multiple_of(i * step, step), step)
-        x = x_all[:, :, at].reshape(total, step)
-        return (
-            carry[0] + jnp.dot(x, w_gate[at, :], preferred_element_type=f32),
-            carry[1] + jnp.dot(x, w_up[at, :], preferred_element_type=f32),
-        )
-
-    zeros = jnp.zeros((total, hidden), f32)
-    gate_proj, up_proj = lax.fori_loop(0, D // step, project, (zeros, zeros))
-    lanes = lax.broadcasted_iota(jnp.int32, (total, 128), 1)
-    scaled = jnp.sum(
-        jnp.where(lanes == me // 2, gates[...].reshape(total, 128), 0.0), -1, keepdims=True
-    )
-    activated = (gate_proj / (1.0 + jnp.exp(-gate_proj)) * up_proj * scaled).astype(bf16)
-
-    weights[2].wait()
+    lanes_of = lax.broadcasted_iota(jnp.int32, (total, 128), 1)
+
+    def activate(x_ref, gates_ref):
+        both = jnp.dot(x_ref[...].reshape(total, D), w_in[...], preferred_element_type=f32)
+        gate_proj, up_proj = both[:, :hidden], both[:, hidden:]
+        scaled = jnp.sum(
+            jnp.where(lanes_of == me // 2, gates_ref[...].reshape(total, 128), 0.0),
+            -1,
+            keepdims=True,
+        )
+        return (gate_proj / (1.0 + jnp.exp(-gate_proj)) * up_proj * scaled).astype(bf16)
+
     chunks = c_sem.shape[1]
     width = D // chunks
 
@@ -532,8 +665,8 @@
 
     def core_copy(i):
         return remote(
-            part.at[1 - core, :, :, :, cut(i)],
-            core_recv.at[:, :, :, cut(i)],
+            part_a.at[1 - core, :, :, old_rows, cut(i)],
+            core_a.at[:, :, old_rows, cut(i)],
             c_sem.at[0, i],
             c_sem.at[1, i],
             other_core,
@@ -541,8 +674,8 @@
 
     def row_copy(i):
         return remote(
-            y_send.at[:, :, cut(i)],
-            y_recv.at[:, :, cut(i)],
+            y_send.at[:, old_rows, cut(i)],
+            y_recv.at[:, old_rows, cut(i)],
             y_sem.at[0, i],
             y_sem.at[1, i],
             other_row,
@@ -551,31 +684,42 @@
     def line_copy(i, k):
         to = lax.rem(line + k, lines)
         return remote(
-            z_send.at[k, :, cut(i)],
-            z_recv.at[k, :, cut(i)],
+            z_send.at[k, old_rows, cut(i)],
+            z_recv.at[k, old_rows, cut(i)],
             zs_sem.at[k, i],
             zr_sem.at[k, i],
             device(to, row, core),
         )
 
+    activated = activate(x_a, gates_a)
     for i in range(chunks):
         rows = jnp.dot(activated, w_down[:, cut(i)], preferred_element_type=f32)
-        part[:, :, :, :, cut(i)] = rows.astype(bf16).reshape(2, 2, lines, seqs, width)
+        part_a[:, :, :, :, cut(i)] = rows.astype(bf16).reshape(2, 2, lines, seqs, width)
         core_copy(i).start()
+
+    def b_pass(k, carry):
+        for pool in b_pools:
+            b_copy(pool, k).wait_recv()
+            b_forward(pool, k).start()
+        return carry
+
     for i in range(chunks):
         core_copy(i).wait()
         y_send[:, :, cut(i)] = (
-            part[core, 1 - row, :, :, cut(i)].astype(f32)
-            + core_recv[1 - row, :, :, cut(i)].astype(f32)
+            part_a[core, 1 - row, :, :, cut(i)].astype(f32)
+            + core_a[1 - row, :, :, cut(i)].astype(f32)
         ).astype(bf16)
         row_copy(i).start()
+
+    lax.fori_loop(1, chips, b_pass, 0)
+
     for i in range(chunks):
         row_copy(i).wait()
 
         def summed(at_line):
             return (
-                part[core, row, at_line, :, cut(i)].astype(f32)
-                + core_recv[row, at_line, :, cut(i)].astype(f32)
+                part_a[core, row, at_line, :, cut(i)].astype(f32)
+                + core_a[row, at_line, :, cut(i)].astype(f32)
                 + y_recv[at_line, :, cut(i)].astype(f32)
             )
 
@@ -583,14 +727,86 @@
             z_send[k, :, cut(i)] = summed(lax.rem(line + k, lines)).astype(bf16)
             line_copy(i, k).start()
         kept[:, cut(i)] = attn[:, cut(i)] + summed(line)
-    for i in range(chunks):
-        answer = kept[:, cut(i)]
-        for k in range(1, lines):
+
+    def b_arrive(k, carry):
+        for pool in b_pools:
+            b_forward(pool, k).wait()
+        return carry
+
+    lax.fori_loop(0, chips, b_arrive, 0)
+    activated = activate(x_b, gates_b)
+    b_chunks = cb_sem.shape[1]
+    b_width = D // b_chunks
+
+    def b_core(i):
+        at = slice(i * b_width, (i + 1) * b_width)
+        return remote(
+            part_b.at[1 - core, :, new_rows, at],
+            core_b.at[:, new_rows, at],
+            cb_sem.at[0, i],
+            cb_sem.at[1, i],
+            other_core,
+        )
+
+    for i in range(b_chunks):
+        at = slice(i * b_width, (i + 1) * b_width)
+        rows = jnp.dot(activated, w_down[:, at], preferred_element_type=f32)
+        part_b[:, :, :, at] = rows.astype(bf16).reshape(2, chips, seqs, b_width)
+        b_core(i).start()
+
+    def b_return(k):
+        to = lax.rem(unit + k, chips)
+        return remote(
+            sum_b.at[to, new_rows],
+            recv_b.at[unit, new_rows],
+            rb_sem.at[0, k],
+            rb_sem.at[1, k],
+            device_of(to, core),
+        )
+
+    for i in range(b_chunks):
+        b_core(i).wait()
+
+    def b_sum(k, carry):
+        to = lax.rem(unit + k, chips)
+        sum_b[to] = (part_b[core, to].astype(f32) + core_b[to].astype(f32)).astype(bf16)
+        b_return(k).start()
+        return carry
+
+    lax.fori_loop(1, chips, b_sum, 0)
+    last = attn[...] + part_b[core, unit].astype(f32) + core_b[unit].astype(f32)
+
+    answer = kept[...]
+    for k in range(1, lines):
+        for i in range(chunks):
             line_copy(i, k).wait()
-            answer = answer + z_recv[k, :, cut(i)].astype(f32)
-        out_ref[:, cut(i)] = answer.astype(bf16)
+        answer = answer + z_recv[k].astype(f32)
+
+    def b_last(k, total):
+        b_return(k).wait()
+        return total + recv_b[lax.rem(unit + chips - k, chips)].astype(f32)
+
+    for k in range(1, chips):
+        last = b_last(k, last)
+    is_b = lax.broadcasted_iota(jnp.int32, (seqs, D), 0) < MAXP
+    out_ref[...] = jnp.where(is_b, last, answer).astype(bf16)
+    out_copy = pltpu.make_async_copy(out_ref, out_hbm, out_sem)
+    out_copy.start()
+
+    page_copy.wait_send()
     for copy in sent:
         copy.wait_send()
+
+    def drain(k, carry):
+        q_copy(k).wait_send()
+        for copy in o_copy(k):
+            copy.wait_send()
+        for pool in b_pools:
+            b_copy(pool, k).wait_send()
+        return carry
+
+    lax.fori_loop(1, chips, drain, 0)
+    out_copy.wait()
 
 
 def dense(
@@ -614,9 +830,11 @@
     seqs = hidden_in.shape[0]
     hidden = w_gate.shape[2]
     lines = devices // 4
+    chips = devices // 2
     bf16, f32 = jnp.bfloat16, jnp.float32
-    chunks = 8
-    pieces = 2
+    chunks = 4
+    b_chunks = 2
+    packed = D * MAXP // seqs
     loaded = (
         prompt_kv[0],
         queries,
@@ -629,23 +847,27 @@
         route_ids,
     )
     smem = pl.BlockSpec(memory_space=pltpu.SMEM)
-    vmem = pl.BlockSpec(memory_space=pltpu.VMEM)
     hbm = pl.BlockSpec(memory_space=pltpu.HBM)
     dma = pltpu.SemaphoreType.DMA
-    page = (MAXP, 2, PAGE_TOKENS, KEY_VALUE_HEADS * HEAD_SIZE)
     return pl.pallas_call(
         functools.partial(layer_kernel, devices),
         out_shape=jax.ShapeDtypeStruct((seqs, D), bf16),
         in_specs=[smem] * 3 + [hbm] * (len(loaded) + 3),
-        out_specs=vmem,
+        out_specs=hbm,
         scratch_shapes=[pltpu.VMEM(a.shape, a.dtype) for a in loaded]
         + [
-            pltpu.VMEM((D, hidden), bf16),
-            pltpu.VMEM((D, hidden), bf16),
+            pltpu.VMEM((D, 2 * hidden), bf16),
             pltpu.VMEM((hidden, D), bf16),
-            pltpu.VMEM((devices,) + page, bf16),
-            pltpu.VMEM((devices,) + page, bf16),
+            pltpu.VMEM(loaded[0].shape, bf16),
+            pltpu.VMEM((seqs, packed), bf16),
+            pltpu.VMEM((chips, seqs, packed), bf16),
+            pltpu.VMEM((chips, seqs, packed), bf16),
+            pltpu.VMEM((chips, seqs, packed), bf16),
+            pltpu.VMEM((chips, seqs, 128), f32),
+            pltpu.VMEM((chips, seqs, 128), f32),
             pltpu.VMEM((seqs, D), f32),
+            pltpu.VMEM((devices, seqs, D), bf16),
+            pltpu.VMEM((devices, seqs, 128), f32),
             pltpu.VMEM((devices, seqs, D), bf16),
             pltpu.VMEM((devices, seqs, 128), f32),
             pltpu.VMEM((2, 2, lines, seqs, D), bf16),
@@ -655,16 +877,28 @@
             pltpu.VMEM((lines, seqs, D), bf16),
             pltpu.VMEM((lines, seqs, D), bf16),
             pltpu.VMEM((seqs, D), f32),
+            pltpu.VMEM((2, chips, seqs, D), bf16),
+            pltpu.VMEM((chips, seqs, D), bf16),
+            pltpu.VMEM((chips, seqs, D), bf16),
+            pltpu.VMEM((chips, seqs, D), bf16),
+            pltpu.VMEM((seqs, D), bf16),
             dma((len(loaded),)),
             dma((3,)),
-            dma((devices,)),
-            dma((devices,)),
-            dma((pieces + 1, 4 * lines)),
-            dma((pieces + 1, devices)),
+            dma((2,)),
+            dma((2, chips)),
+            dma((2, chips)),
+            dma((2, chips)),
+            dma((2, 4 * lines)),
+            dma((2, devices)),
+            dma((2, 2, chips)),
+            dma((2, 2, chips)),
             dma((2, chunks)),
             dma((2, chunks)),
             dma((lines, chunks)),
             dma((lines, chunks)),
+            dma((2, b_chunks)),
+            dma((2, chips)),
+            dma(()),
         ],
         compiler_params=pltpu.CompilerParams(
             collective_id=0, has_side_effects=True, vmem_limit_bytes=67043328

time: 52.7 us -> 44.2 us (0.84)
  Pallas kernels: 51 us -> 42.6 us
    pallas_call x1, Pallas kernels: 51 us -> 42.6 us  [dense(): pl.pallas_call(functools.partial(layer_kernel, devices), out_shape=jax.Sh...]
where the time goes in v1:
time: 44.2 us; the launch traced here: 44.1 us
  Pallas kernels  42.6 us (96%)
  local copies, waits for them, and re-layouts  1.47 us (3%)
    pallas_call x1, Pallas kernels, dense(): pl.pallas_call(functools.partial(layer_kernel, devices), out_shape=jax.Sh...  42.6 us
    unnamed x1, local copies, waits for them, and re-layouts  1.47 us

profile of v1, /device:TPU:0, one launch (start us, length us, event | category | flops | bytes accessed | tf_op | source)
XLA Modules:
  0.0 44.1 jit_solution(3421132015215848654)
XLA Ops:
  0.0 42.6 %shard_map.145 = bf16[8,4096]{1,0:T(8,128)(2,1)} custom-call(s32[16]{0:T(128)} %owners.1, s32[16]{0:T(128)} %prompt_lengths.1, s32[8]{0:T(128)} %blocks.1, bf16[16,2,16,256]{3,2,1,0:T(8,128)(2,1)} %bitcast.3, bf16[8,4096]{1,0:T(8,128)(2,1)} %q_hbm.1, bf16[8,2,256]{2,1,0:T(2,128)(2,1)} %dkv_hbm.1, s32[8,16]{1,0:T(8,128)} %table_hbm.1, ...), custom_call_target="tpu_custom_call" | custom-call | tf_op jit(solution)/shard_map/pallas_call | solution.py:852
  42.6 1.5 %copy.17 = bf16[8,4096]{1,0:T(8,128)(2,1)} copy(bf16[8,4096]{1,0:T(8,128)(2,1)} %shard_map.145) | data formatting | bytes 131072

commit v2 on v1

--- a/solution.py
+++ b/solution.py
@@ -189,9 +189,9 @@
 
 def layer_kernel(
     devices,
-    owners,
-    prompt_lengths,
-    blocks,
+    owners_hbm,
+    lengths_hbm,
+    blocks_hbm,
     pages_hbm,
     q_hbm,
     dkv_hbm,
@@ -204,7 +204,10 @@
     gate_hbm,
     up_hbm,
     down_hbm,
-    out_hbm,
+    out_ref,
+    owners,
+    prompt_lengths,
+    blocks,
     pages_ref,
     q_ref,
     dkv_ref,
@@ -239,7 +242,6 @@
     core_b,
     sum_b,
     recv_b,
-    out_ref,
     in_sem,
     w_sem,
     page_sem,
@@ -248,15 +250,16 @@
     lse_sem,
     xa_ssem,
     xa_rsem,
-    xb_sem,
-    xf_sem,
-    c_sem,
-    y_sem,
-    zs_sem,
-    zr_sem,
-    cb_sem,
+    xb_ssem,
+    xb_rsem,
+    c_ssem,
+    c_rsem,
+    y_ssem,
+    y_rsem,
+    z_sem,
+    cb_ssem,
+    cb_rsem,
     rb_sem,
-    out_sem,
 ):
     f32, bf16 = jnp.float32, jnp.bfloat16
     me = lax.axis_index("expert")
@@ -278,6 +281,23 @@
 
     def place(at_line, at_row, at_core):
         return (at_core * 2 + at_row) * lines + at_line
+
+    low = line * 2 < lines
+
+    def far_line(j):
+        return jnp.where(low, lines - 1 - j, j)
+
+    def far_other_line(j):
+        down = lines - 1 - j
+        return jnp.where(
+            low, jnp.where(down > line, down, down - 1), jnp.where(j < line, j, j + 1)
+        )
+
+    def other_units():
+        for j in range(lines):
+            yield (1 - row) * lines + far_line(j)
+            if j < lines - 1:
+                yield row * lines + far_other_line(j)
 
     def remote(src, dst, ssem, rsem, to):
         return pltpu.make_async_remote_copy(
@@ -306,6 +326,9 @@
                 (gain_hbm, gain_ref),
                 (router_hbm, router_ref),
                 (ids_hbm, ids_ref),
+                (blocks_hbm, blocks),
+                (owners_hbm, owners),
+                (lengths_hbm, prompt_lengths),
             )
         )
     ]
@@ -368,15 +391,11 @@
     q_send[...] = q_packed.astype(bf16)
     pl.semaphore_wait(barrier, devices - 1)
 
-    def q_copy(k):
-        to = device_of(lax.rem(unit + k, chips), core)
-        return remote(q_send, q_recv.at[unit], q_sem.at[0, k], q_sem.at[1, k], to)
-
-    def q_go(k, carry):
-        q_copy(k).start()
-        return carry
-
-    lax.fori_loop(1, chips, q_go, 0)
+    def q_copy(to):
+        return remote(q_send, q_recv.at[unit], q_sem.at[0], q_sem.at[1], device_of(to, core))
+
+    for to in other_units():
+        q_copy(to).start()
     q_recv[unit] = q_packed.astype(bf16)
     loads[1].wait()
     page_copy = remote(pages_ref, other_pages, page_sem.at[0], page_sem.at[1], other_core)
@@ -448,28 +467,34 @@
     normed = norm_of(residual_of(attn[...]))
     x_a[mine] = normed
 
-    def pass_on(pool, spot, at, to):
+    def pass_on(pool, spot, count, at, to):
         buffer, rows, n = pool
-        ref = buffer.at[spot, rows]
-        return remote(ref, ref, xa_ssem.at[n, at], xa_rsem.at[n, spot], to)
+        ref = buffer.at[pl.ds(spot, count), rows]
+        return remote(ref, ref, xa_ssem.at[n], xa_rsem.at[n, at], to)
+
+    at_y, at_core = lines - 1, (lines, lines + 1)
+    row_spots = [(core * 2 + at_row) * lines for at_row in (row, 1 - row)]
+
+    def z_copy(pool, k):
+        return pass_on(pool, mine, 1, k - 1, device(lax.rem(line + k, lines), row, core))
+
+    def z_arrive(pool, k):
+        spot = place(lax.rem(line + lines - k, lines), row, core)
+        pass_on(pool, spot, 1, k - 1, other_row).wait_recv()
+        pass_on(pool, spot, 1, at_y, other_row).start()
+
+    def over_core(pool, n):
+        pass_on(pool, row_spots[n], lines, at_core[n], other_core).start()
 
     def first_hops(pool):
-        copies = []
         for k in range(1, lines):
-            copies.append(pass_on(pool, mine, k, device(lax.rem(line + k, lines), row, core)))
-        copies.append(pass_on(pool, mine, 0, other_row))
-        copies.append(pass_on(pool, mine, lines, other_core))
-        for copy in copies:
-            copy.start()
-        return copies
-
-    def arrived(pool, spot):
-        pass_on(pool, spot, 0, other_core).wait_recv()
+            z_copy(pool, k).start()
+        pass_on(pool, mine, 1, at_y, other_row).start()
 
     pools = [(x_a, old_rows, 0), (gates_a, pl.ds(0, seqs), 1)]
-    sent = first_hops(pools[0])
+    first_hops(pools[0])
     gates_a[mine] = gate_of(normed)
-    sent += first_hops(pools[1])
+    first_hops(pools[1])
 
     prompts = owners.shape[0]
     shape = (1, prompts * PAGE_TOKENS)
@@ -494,11 +519,9 @@
     allowed = (allowed_at(me), allowed_at(other_core))
     page_copy.wait_recv()
 
-    def q_end(k, carry):
-        q_copy(k).wait_recv()
-        return carry
-
-    lax.fori_loop(1, chips, q_end, 0)
+    few = pl.ds(0, chips - 1)
+    q_all = remote(q_recv.at[few], q_recv.at[few], q_sem.at[0], q_sem.at[1], other_core)
+    q_all.wait_recv()
     lane_of = lax.broadcasted_iota(jnp.int32, (slots, 128), 1)
     lse_all = jnp.zeros((slots, 128), f32)
     for h in range(KEY_VALUE_HEADS):
@@ -531,40 +554,24 @@
             lse_all = jnp.where(lane_of == hh, lse[rows], lse_all)
     lse_send[...] = lse_all.reshape(chips, seqs, 128)
 
-    def o_copy(k):
-        to = lax.rem(unit + k, chips)
+    def o_copy(to):
         at = device_of(to, core)
         return (
-            remote(o_send.at[to], o_recv.at[unit], o_sem.at[0, k], o_sem.at[1, k], at),
-            remote(lse_send.at[to], lse_recv.at[unit], lse_sem.at[0, k], lse_sem.at[1, k], at),
-        )
-
-    def o_go(k, carry):
-        for copy in o_copy(k):
+            remote(o_send.at[to], o_recv.at[unit], o_sem.at[0], o_sem.at[1], at),
+            remote(lse_send.at[to], lse_recv.at[unit], lse_sem.at[0], lse_sem.at[1], at),
+        )
+
+    for to in other_units():
+        for copy in o_copy(to):
             copy.start()
-        return carry
-
-    lax.fori_loop(1, chips, o_go, 0)
     o_recv[unit] = o_send[unit]
     lse_recv[unit] = lse_send[unit]
 
-    def over_core(k):
-        spot = place(lax.rem(line + k, lines), 1 - row, core)
+    for k in range(1, lines):
         for pool in pools:
-            arrived(pool, spot)
-            copy = pass_on(pool, spot, 3 * lines - 1 + k, other_core)
-            copy.start()
-            sent.append(copy)
-
-    over_core(0)
-    for k in range(1, lines):
-        spot = place(lax.rem(line + k, lines), row, core)
-        for pool in pools:
-            arrived(pool, spot)
-            for step, to in ((0, other_row), (1, other_core)):
-                copy = pass_on(pool, spot, lines + 2 * k - 1 + step, to)
-                copy.start()
-                sent.append(copy)
+            z_arrive(pool, k)
+    for pool in pools:
+        over_core(pool, 0)
 
     own_both = dkv_ref[...].astype(f32)
     own_key = spread_rows(own_both[:, 0])
@@ -581,12 +588,12 @@
         new_count = new_count + (owners[p] == me).astype(jnp.int32)
     is_new = lax.broadcasted_iota(jnp.int32, (seqs, HEAD_SIZE), 0) < new_count
 
-    def o_end(k, carry):
-        for copy in o_copy(k):
-            copy.wait_recv()
-        return carry
-
-    lax.fori_loop(1, chips, o_end, 0)
+    o_all = (
+        remote(o_recv.at[few], o_recv.at[few], o_sem.at[0], o_sem.at[1], other_core),
+        remote(lse_recv.at[few], lse_recv.at[few], lse_sem.at[0], lse_sem.at[1], other_core),
+    )
+    for copy in o_all:
+        copy.wait_recv()
     peak = own_score
     for u in range(chips):
         peak = jnp.maximum(peak, lse_recv[u])
@@ -613,35 +620,30 @@
 
     b_pools = [(x_b, new_rows, 0), (gates_b, pl.ds(0, seqs), 1)]
 
-    def b_copy(pool, k):
+    def b_copy(pool, to):
         buffer, rows, n = pool
         ref = buffer.at[mine, rows]
-        to = device_of(lax.rem(unit + k, chips), core)
-        return remote(ref, ref, xb_sem.at[0, n, k], xb_sem.at[1, n, k], to)
-
-    def b_forward(pool, k):
+        return remote(ref, ref, xb_ssem.at[n], xb_rsem.at[n, 0], device_of(to, core))
+
+    def b_spots(pool, count, at):
         buffer, rows, n = pool
-        ref = buffer.at[core * chips + lax.rem(unit + chips - k, chips), rows]
-        return remote(ref, ref, xf_sem.at[0, n, k], xf_sem.at[1, n, k], other_core)
+        ref = buffer.at[pl.ds(core * chips, count), rows]
+        return remote(ref, ref, xb_ssem.at[n], xb_rsem.at[n, at], other_core)
 
     def b_first(pool):
-        def go(k, carry):
-            b_copy(pool, k).start()
-            return carry
-
-        lax.fori_loop(1, chips, go, 0)
-        b_forward(pool, 0).start()
+        for to in other_units():
+            b_copy(pool, to).start()
 
     b_first(b_pools[0])
     gates_b[mine] = gate_of(normed)
     b_first(b_pools[1])
 
-    for k in range(1, lines):
-        over_core(k)
-    for at_row in range(2):
-        for k in range(lines):
-            for pool in pools:
-                arrived(pool, place(k, at_row, 1 - core))
+    for pool in pools:
+        pass_on(pool, row_spots[1], lines, at_y, other_row).wait_recv()
+        over_core(pool, 1)
+    for pool in pools:
+        for n in range(2):
+            pass_on(pool, row_spots[n], lines, at_core[n], other_core).wait_recv()
     for copy in weights:
         copy.wait()
     total = devices * seqs
@@ -657,7 +659,7 @@
         )
         return (gate_proj / (1.0 + jnp.exp(-gate_proj)) * up_proj * scaled).astype(bf16)
 
-    chunks = c_sem.shape[1]
+    chunks = c_rsem.shape[0]
     width = D // chunks
 
     def cut(i):
@@ -667,8 +669,8 @@
         return remote(
             part_a.at[1 - core, :, :, old_rows, cut(i)],
             core_a.at[:, :, old_rows, cut(i)],
-            c_sem.at[0, i],
-            c_sem.at[1, i],
+            c_ssem,
+            c_rsem.at[i],
             other_core,
         )
 
@@ -676,8 +678,8 @@
         return remote(
             y_send.at[:, old_rows, cut(i)],
             y_recv.at[:, old_rows, cut(i)],
-            y_sem.at[0, i],
-            y_sem.at[1, i],
+            y_ssem,
+            y_rsem.at[i],
             other_row,
         )
 
@@ -686,8 +688,8 @@
         return remote(
             z_send.at[k, old_rows, cut(i)],
             z_recv.at[k, old_rows, cut(i)],
-            zs_sem.at[k, i],
-            zr_sem.at[k, i],
+            z_sem.at[0],
+            z_sem.at[1],
             device(to, row, core),
         )
 
@@ -697,24 +699,51 @@
         part_a[:, :, :, :, cut(i)] = rows.astype(bf16).reshape(2, 2, lines, seqs, width)
         core_copy(i).start()
 
-    def b_pass(k, carry):
-        for pool in b_pools:
-            b_copy(pool, k).wait_recv()
-            b_forward(pool, k).start()
-        return carry
+    for pool in b_pools:
+        b_spots(pool, chips - 1, 0).wait_recv()
+        b_spots(pool, chips, 1).start()
 
     for i in range(chunks):
-        core_copy(i).wait()
+        core_copy(i).wait_recv()
         y_send[:, :, cut(i)] = (
             part_a[core, 1 - row, :, :, cut(i)].astype(f32)
             + core_a[1 - row, :, :, cut(i)].astype(f32)
         ).astype(bf16)
         row_copy(i).start()
 
-    lax.fori_loop(1, chips, b_pass, 0)
+    for pool in b_pools:
+        b_spots(pool, chips, 1).wait_recv()
+    activated = activate(x_b, gates_b)
+    b_chunks = cb_rsem.shape[0]
+    b_width = D // b_chunks
+
+    def b_core(i):
+        at = slice(i * b_width, (i + 1) * b_width)
+        return remote(
+            part_b.at[1 - core, :, new_rows, at],
+            core_b.at[:, new_rows, at],
+            cb_ssem,
+            cb_rsem.at[i],
+            other_core,
+        )
+
+    for i in range(b_chunks):
+        at = slice(i * b_width, (i + 1) * b_width)
+        rows = jnp.dot(activated, w_down[:, at], preferred_element_type=f32)
+        part_b[:, :, :, at] = rows.astype(bf16).reshape(2, chips, seqs, b_width)
+        b_core(i).start()
+
+    def b_return(to):
+        return remote(
+            sum_b.at[to, new_rows],
+            recv_b.at[unit, new_rows],
+            rb_sem.at[0],
+            rb_sem.at[1],
+            device_of(to, core),
+        )
 
     for i in range(chunks):
-        row_copy(i).wait()
+        row_copy(i).wait_recv()
 
         def summed(at_line):
             return (
@@ -728,85 +757,45 @@
             line_copy(i, k).start()
         kept[:, cut(i)] = attn[:, cut(i)] + summed(line)
 
-    def b_arrive(k, carry):
-        for pool in b_pools:
-            b_forward(pool, k).wait()
-        return carry
-
-    lax.fori_loop(0, chips, b_arrive, 0)
-    activated = activate(x_b, gates_b)
-    b_chunks = cb_sem.shape[1]
-    b_width = D // b_chunks
-
-    def b_core(i):
-        at = slice(i * b_width, (i + 1) * b_width)
-        return remote(
-            part_b.at[1 - core, :, new_rows, at],
-            core_b.at[:, new_rows, at],
-            cb_sem.at[0, i],
-            cb_sem.at[1, i],
-            other_core,
-        )
-
     for i in range(b_chunks):
-        at = slice(i * b_width, (i + 1) * b_width)
-        rows = jnp.dot(activated, w_down[:, at], preferred_element_type=f32)
-        part_b[:, :, :, at] = rows.astype(bf16).reshape(2, chips, seqs, b_width)
-        b_core(i).start()
-
-    def b_return(k):
-        to = lax.rem(unit + k, chips)
-        return remote(
-            sum_b.at[to, new_rows],
-            recv_b.at[unit, new_rows],
-            rb_sem.at[0, k],
-            rb_sem.at[1, k],
-            device_of(to, core),
-        )
-
-    for i in range(b_chunks):
-        b_core(i).wait()
-
-    def b_sum(k, carry):
-        to = lax.rem(unit + k, chips)
+        b_core(i).wait_recv()
+    for to in other_units():
         sum_b[to] = (part_b[core, to].astype(f32) + core_b[to].astype(f32)).astype(bf16)
-        b_return(k).start()
-        return carry
-
-    lax.fori_loop(1, chips, b_sum, 0)
+        b_return(to).start()
     last = attn[...] + part_b[core, unit].astype(f32) + core_b[unit].astype(f32)
 
+    rest = pl.ds(1, lines - 1)
+    z_all = remote(
+        z_recv.at[rest, old_rows], z_recv.at[rest, old_rows], z_sem.at[0], z_sem.at[1], other_core
+    )
+    z_all.wait_recv()
     answer = kept[...]
     for k in range(1, lines):
-        for i in range(chunks):
-            line_copy(i, k).wait()
         answer = answer + z_recv[k].astype(f32)
 
-    def b_last(k, total):
-        b_return(k).wait()
-        return total + recv_b[lax.rem(unit + chips - k, chips)].astype(f32)
-
+    b_all = remote(
+        recv_b.at[few, new_rows], recv_b.at[few, new_rows], rb_sem.at[0], rb_sem.at[1], other_core
+    )
+    b_all.wait_recv()
     for k in range(1, chips):
-        last = b_last(k, last)
+        last = last + recv_b[lax.rem(unit + k, chips)].astype(f32)
     is_b = lax.broadcasted_iota(jnp.int32, (seqs, D), 0) < MAXP
     out_ref[...] = jnp.where(is_b, last, answer).astype(bf16)
-    out_copy = pltpu.make_async_copy(out_ref, out_hbm, out_sem)
-    out_copy.start()
-
-    page_copy.wait_send()
-    for copy in sent:
+
+    for copy in (page_copy, q_all, z_all, b_all) + o_all:
         copy.wait_send()
-
-    def drain(k, carry):
-        q_copy(k).wait_send()
-        for copy in o_copy(k):
-            copy.wait_send()
-        for pool in b_pools:
-            b_copy(pool, k).wait_send()
-        return carry
-
-    lax.fori_loop(1, chips, drain, 0)
-    out_copy.wait()
+    for n, (buffer, rows) in enumerate(((x_a, old_rows), (gates_a, pl.ds(0, seqs)))):
+        ref = buffer.at[pl.ds(0, 4 * lines - 1), rows]
+        remote(ref, ref, xa_ssem.at[n], xa_rsem.at[n, 0], other_core).wait_send()
+    for n, (buffer, rows) in enumerate(((x_b, new_rows), (gates_b, pl.ds(0, seqs)))):
+        ref = buffer.at[pl.ds(0, 2 * chips - 1), rows]
+        remote(ref, ref, xb_ssem.at[n], xb_rsem.at[n, 0], other_core).wait_send()
+    for ref, ssem, rsem in (
+        (part_a.at[0, :, :, old_rows], c_ssem, c_rsem.at[0]),
+        (y_send.at[:, old_rows], y_ssem, y_rsem.at[0]),
+        (part_b.at[0, :, new_rows], cb_ssem, cb_rsem.at[0]),
+    ):
+        remote(ref, ref, ssem, rsem, other_core).wait_send()
 
 
 def dense(
@@ -846,15 +835,16 @@
         router.T,
         route_ids,
     )
-    smem = pl.BlockSpec(memory_space=pltpu.SMEM)
+    scalars = (prompt_owner, prompt_pages, seq_blocks)
     hbm = pl.BlockSpec(memory_space=pltpu.HBM)
     dma = pltpu.SemaphoreType.DMA
     return pl.pallas_call(
         functools.partial(layer_kernel, devices),
-        out_shape=jax.ShapeDtypeStruct((seqs, D), bf16),
-        in_specs=[smem] * 3 + [hbm] * (len(loaded) + 3),
-        out_specs=hbm,
-        scratch_shapes=[pltpu.VMEM(a.shape, a.dtype) for a in loaded]
+        out_shape=pltpu.VMEM((seqs, D), bf16),
+        in_specs=[hbm] * (len(loaded) + 6),
+        out_specs=pl.BlockSpec(memory_space=pltpu.VMEM),
+        scratch_shapes=[pltpu.SMEM(a.shape, a.dtype) for a in scalars]
+        + [pltpu.VMEM(a.shape, a.dtype) for a in loaded]
         + [
             pltpu.VMEM((D, 2 * hidden), bf16),
             pltpu.VMEM((hidden, D), bf16),
@@ -881,29 +871,29 @@
             pltpu.VMEM((chips, seqs, D), bf16),
             pltpu.VMEM((chips, seqs, D), bf16),
             pltpu.VMEM((chips, seqs, D), bf16),
-            pltpu.VMEM((seqs, D), bf16),
-            dma((len(loaded),)),
+            dma((len(loaded) + len(scalars),)),
             dma((3,)),
             dma((2,)),
-            dma((2, chips)),
-            dma((2, chips)),
-            dma((2, chips)),
-            dma((2, 4 * lines)),
-            dma((2, devices)),
-            dma((2, 2, chips)),
-            dma((2, 2, chips)),
-            dma((2, chunks)),
-            dma((2, chunks)),
-            dma((lines, chunks)),
-            dma((lines, chunks)),
-            dma((2, b_chunks)),
-            dma((2, chips)),
+            dma((2,)),
+            dma((2,)),
+            dma((2,)),
+            dma((2,)),
+            dma((2, lines + 2)),
+            dma((2,)),
+            dma((2, 2)),
             dma(()),
+            dma((chunks,)),
+            dma(()),
+            dma((chunks,)),
+            dma((2,)),
+            dma(()),
+            dma((b_chunks,)),
+            dma((2,)),
         ],
         compiler_params=pltpu.CompilerParams(
-            collective_id=0, has_side_effects=True, vmem_limit_bytes=67043328
+            collective_id=0, has_side_effects=True, vmem_limit_bytes=58 * 2**20
         ),
-    )(prompt_owner, prompt_pages, seq_blocks, *loaded, w_gate, w_up, w_down)
+    )(*scalars, *loaded, w_gate, w_up, w_down)
 
 
 def local(*arrays):

time: 44.2 us -> 39.1 us (0.88)
  Pallas kernels: 42.6 us -> 38.3 us
  local copies, waits for them, and re-layouts: 1.47 us -> 0.63 us
    pallas_call x1, Pallas kernels: 42.6 us -> 38.3 us  [dense(): pl.pallas_call(functools.partial(layer_kernel, devices), out_shape=pltpu....]
    unnamed x1, local copies, waits for them, and re-layouts: 1.47 us -> 0.63 us
where the time goes in v2:
time: 39.1 us; the launch traced here: 39 us
  Pallas kernels  38.3 us (98%)
  local copies, waits for them, and re-layouts  0.63 us (2%)
    pallas_call x1, Pallas kernels, dense(): pl.pallas_call(functools.partial(layer_kernel, devices), out_shape=pltpu....  38.3 us

profile of v2, /device:TPU:0, one launch (start us, length us, event | category | flops | bytes accessed | tf_op | source)
XLA Modules:
  0.0 39.0 jit_solution(12879354714894881068)
XLA Ops:
  0.0 38.3 %shard_map.145 = bf16[8,4096]{1,0:T(8,128)(2,1)S(1)} custom-call(s32[16]{0:T(128)} %owners_hbm.1, s32[16]{0:T(128)} %lengths_hbm.1, s32[8]{0:T(128)} %blocks_hbm.1, bf16[16,2,16,256]{3,2,1,0:T(8,128)(2,1)} %bitcast.3, bf16[8,4096]{1,0:T(8,128)(2,1)} %q_hbm.1, bf16[8,2,256]{2,1,0:T(2,128)(2,1)} %dkv_hbm.1, s32[8,16]{1,0:T(8,128)} %table_hbm.1, ...), custom_call_target="tpu_custom_call" | custom-call | tf_op jit(solution)/shard_map/pallas_call | solution.py:841
  38.3 0.6 %copy.17 = bf16[8,4096]{1,0:T(8,128)(2,1)} copy(bf16[8,4096]{1,0:T(8,128)(2,1)S(1)} %shard_map.145) | data formatting | bytes 131072

commit v3 on v2

--- a/solution.py
+++ b/solution.py
@@ -237,6 +237,10 @@
     y_recv,
     z_send,
     z_recv,
+    zf_send,
+    zf_recv,
+    yf_send,
+    yf_recv,
     kept,
     part_b,
     core_b,
@@ -257,6 +261,9 @@
     y_ssem,
     y_rsem,
     z_sem,
+    zf_ssem,
+    zf_rsem,
+    yf_sem,
     cb_ssem,
     cb_rsem,
     rb_sem,
@@ -292,6 +299,10 @@
         return jnp.where(
             low, jnp.where(down > line, down, down - 1), jnp.where(j < line, j, j + 1)
         )
+
+    def all_units():
+        yield from other_units()
+        yield unit
 
     def other_units():
         for j in range(lines):
@@ -389,18 +400,6 @@
     loads[0].wait()
     q_packed = pack(q_ref[...].astype(f32))
     q_send[...] = q_packed.astype(bf16)
-    pl.semaphore_wait(barrier, devices - 1)
-
-    def q_copy(to):
-        return remote(q_send, q_recv.at[unit], q_sem.at[0], q_sem.at[1], device_of(to, core))
-
-    for to in other_units():
-        q_copy(to).start()
-    q_recv[unit] = q_packed.astype(bf16)
-    loads[1].wait()
-    page_copy = remote(pages_ref, other_pages, page_sem.at[0], page_sem.at[1], other_core)
-    page_copy.start()
-
     for copy in loads[2:]:
         copy.wait()
 
@@ -466,30 +465,53 @@
 
     normed = norm_of(residual_of(attn[...]))
     x_a[mine] = normed
+    pl.semaphore_wait(barrier, devices - 1)
+
+    def q_copy(to):
+        return remote(q_send, q_recv.at[unit], q_sem.at[0], q_sem.at[1], device_of(to, 1 - core))
+
+    for to in all_units():
+        q_copy(to).start()
+    loads[1].wait()
+    page_copy = remote(pages_ref, other_pages, page_sem.at[0], page_sem.at[1], other_core)
+    page_copy.start()
+
 
     def pass_on(pool, spot, count, at, to):
         buffer, rows, n = pool
         ref = buffer.at[pl.ds(spot, count), rows]
         return remote(ref, ref, xa_ssem.at[n], xa_rsem.at[n, at], to)
 
-    at_y, at_core = lines - 1, (lines, lines + 1)
-    row_spots = [(core * 2 + at_row) * lines for at_row in (row, 1 - row)]
-
-    def z_copy(pool, k):
-        return pass_on(pool, mine, 1, k - 1, device(lax.rem(line + k, lines), row, core))
-
-    def z_arrive(pool, k):
-        spot = place(lax.rem(line + lines - k, lines), row, core)
-        pass_on(pool, spot, 1, k - 1, other_row).wait_recv()
-        pass_on(pool, spot, 1, at_y, other_row).start()
-
-    def over_core(pool, n):
-        pass_on(pool, row_spots[n], lines, at_core[n], other_core).start()
+    far, near = lax.rem(line + 2, lines), line + 1 - 2 * lax.rem(line, 2)
+    far_device, near_device = device(far, row, 1 - core), device(near, row, 1 - core)
+    row_device = device(line, 1 - row, 1 - core)
+    at_far, at_near, at_relay, at_core = 0, 1, 2, 7
+    sources = (far, near, lax.rem(near + 2, lines), line)
+    z_cores, y_cores = (1 - core, 1 - core, core), (core, core, 1 - core, 1 - core)
+
+    def at_y(n):
+        return 3 + n
+
+    def cross(pool, spot, n):
+        pass_on(pool, spot, 1, at_y(n), row_device).start()
+        pass_on(pool, spot, 1, at_core, other_core).start()
+
+    def z_arrive(pool, n):
+        spot = place(sources[n], row, z_cores[n])
+        pass_on(pool, spot, 1, n, other_row).wait_recv()
+        if n == at_far:
+            pass_on(pool, spot, 1, at_relay, near_device).start()
+        cross(pool, spot, n)
+
+    def y_arrive(pool, n):
+        spot = place(sources[n], 1 - row, y_cores[n])
+        pass_on(pool, spot, 1, at_y(n), other_row).wait_recv()
+        pass_on(pool, spot, 1, at_core, other_core).start()
 
     def first_hops(pool):
-        for k in range(1, lines):
-            z_copy(pool, k).start()
-        pass_on(pool, mine, 1, at_y, other_row).start()
+        pass_on(pool, mine, 1, at_far, far_device).start()
+        pass_on(pool, mine, 1, at_near, near_device).start()
+        cross(pool, mine, 3)
 
     pools = [(x_a, old_rows, 0), (gates_a, pl.ds(0, seqs), 1)]
     first_hops(pools[0])
@@ -509,7 +531,7 @@
     slots = chips * seqs
     at_row = lax.broadcasted_iota(jnp.int32, (slots, 1), 0)
     row_unit = at_row // seqs
-    row_owner = device_of(row_unit, core)
+    row_owner = device_of(row_unit, 1 - core)
     match = (owner_of == row_owner) & (rank_of == lax.rem(at_row, MAXP))
 
     def allowed_at(position):
@@ -519,8 +541,7 @@
     allowed = (allowed_at(me), allowed_at(other_core))
     page_copy.wait_recv()
 
-    few = pl.ds(0, chips - 1)
-    q_all = remote(q_recv.at[few], q_recv.at[few], q_sem.at[0], q_sem.at[1], other_core)
+    q_all = remote(q_recv, q_recv, q_sem.at[0], q_sem.at[1], other_core)
     q_all.wait_recv()
     lane_of = lax.broadcasted_iota(jnp.int32, (slots, 128), 1)
     lse_all = jnp.zeros((slots, 128), f32)
@@ -539,15 +560,13 @@
         )
         total = jnp.zeros((slots * per_kv, 1), f32)
         mixed = jnp.zeros((slots * per_kv, HEAD_SIZE), f32)
-        for ref, ok, score in zip((pages_ref, other_pages), allowed, scores):
-            weight = ok * jnp.exp(score - peak)
+        for ref, score in zip((pages_ref, other_pages), scores):
+            weight = jnp.exp(score - peak)
             total = total + jnp.sum(weight, -1, keepdims=True)
             values = ref[:, 1, :, at].reshape(prompts * PAGE_TOKENS, HEAD_SIZE)
             mixed = mixed + jnp.dot(weight.astype(bf16), values, preferred_element_type=f32)
-        some = total > 0
-        safe = jnp.where(some, total, 1.0)
-        mixed = mixed / safe
-        lse = jnp.where(some, peak + jnp.log(safe), masked_score)
+        mixed = mixed / total
+        lse = jnp.where(peak > masked_score, peak + jnp.log(total), masked_score)
         for j, hh in enumerate(lanes):
             rows = slice(j * slots, (j + 1) * slots)
             o_send[:, :, head_cols(hh)] = mixed[rows].astype(bf16).reshape(chips, seqs, HEAD_SIZE)
@@ -555,23 +574,24 @@
     lse_send[...] = lse_all.reshape(chips, seqs, 128)
 
     def o_copy(to):
-        at = device_of(to, core)
+        at = device_of(to, 1 - core)
         return (
             remote(o_send.at[to], o_recv.at[unit], o_sem.at[0], o_sem.at[1], at),
             remote(lse_send.at[to], lse_recv.at[unit], lse_sem.at[0], lse_sem.at[1], at),
         )
 
-    for to in other_units():
+    for to in all_units():
         for copy in o_copy(to):
             copy.start()
-    o_recv[unit] = o_send[unit]
-    lse_recv[unit] = lse_send[unit]
-
-    for k in range(1, lines):
-        for pool in pools:
-            z_arrive(pool, k)
+
     for pool in pools:
-        over_core(pool, 0)
+        z_arrive(pool, at_far)
+    for pool in pools:
+        z_arrive(pool, at_near)
+    for pool in pools:
+        y_arrive(pool, 3)
+    for pool in pools:
+        z_arrive(pool, at_relay)
 
     own_both = dkv_ref[...].astype(f32)
     own_key = spread_rows(own_both[:, 0])
@@ -589,8 +609,8 @@
     is_new = lax.broadcasted_iota(jnp.int32, (seqs, HEAD_SIZE), 0) < new_count
 
     o_all = (
-        remote(o_recv.at[few], o_recv.at[few], o_sem.at[0], o_sem.at[1], other_core),
-        remote(lse_recv.at[few], lse_recv.at[few], lse_sem.at[0], lse_sem.at[1], other_core),
+        remote(o_recv, o_recv, o_sem.at[0], o_sem.at[1], other_core),
+        remote(lse_recv, lse_recv, lse_sem.at[0], lse_sem.at[1], other_core),
     )
     for copy in o_all:
         copy.wait_recv()
@@ -623,47 +643,55 @@
     def b_copy(pool, to):
         buffer, rows, n = pool
         ref = buffer.at[mine, rows]
-        return remote(ref, ref, xb_ssem.at[n], xb_rsem.at[n, 0], device_of(to, core))
-
-    def b_spots(pool, count, at):
+        return remote(ref, ref, xb_ssem.at[n], xb_rsem.at[n, 0], device_of(to, 1 - core))
+
+    def b_core_copy(pool, spot, count):
         buffer, rows, n = pool
-        ref = buffer.at[pl.ds(core * chips, count), rows]
-        return remote(ref, ref, xb_ssem.at[n], xb_rsem.at[n, at], other_core)
+        ref = buffer.at[pl.ds(spot, count), rows]
+        return remote(ref, ref, xb_ssem.at[n], xb_rsem.at[n, 1], other_core)
 
     def b_first(pool):
         for to in other_units():
             b_copy(pool, to).start()
+        b_core_copy(pool, mine, 1).start()
+
+    def b_pass(pool):
+        buffer, rows, n = pool
+        ref = buffer.at[pl.ds(0, chips - 1), rows]
+        remote(ref, ref, xb_ssem.at[n], xb_rsem.at[n, 0], other_core).wait_recv()
+        for source in other_units():
+            b_core_copy(pool, (1 - core) * chips + source, 1).start()
 
     b_first(b_pools[0])
     gates_b[mine] = gate_of(normed)
     b_first(b_pools[1])
 
-    for pool in pools:
-        pass_on(pool, row_spots[1], lines, at_y, other_row).wait_recv()
-        over_core(pool, 1)
-    for pool in pools:
-        for n in range(2):
-            pass_on(pool, row_spots[n], lines, at_core[n], other_core).wait_recv()
     for copy in weights:
         copy.wait()
+
+    def activate(x, gate):
+        total = x.shape[0]
+        lanes_of = lax.broadcasted_iota(jnp.int32, (total, 128), 1)
+        both = jnp.dot(x, w_in[...], preferred_element_type=f32)
+        gate_proj, up_proj = both[:, :hidden], both[:, hidden:]
+        scaled = jnp.sum(jnp.where(lanes_of == me // 2, gate, 0.0), -1, keepdims=True)
+        return (gate_proj / (1.0 + jnp.exp(-gate_proj)) * up_proj * scaled).astype(bf16)
+
     total = devices * seqs
-    lanes_of = lax.broadcasted_iota(jnp.int32, (total, 128), 1)
-
-    def activate(x_ref, gates_ref):
-        both = jnp.dot(x_ref[...].reshape(total, D), w_in[...], preferred_element_type=f32)
-        gate_proj, up_proj = both[:, :hidden], both[:, hidden:]
-        scaled = jnp.sum(
-            jnp.where(lanes_of == me // 2, gates_ref[...].reshape(total, 128), 0.0),
-            -1,
-            keepdims=True,
-        )
-        return (gate_proj / (1.0 + jnp.exp(-gate_proj)) * up_proj * scaled).astype(bf16)
+
+    def rows_of(ref):
+        return ref[...].reshape(total, ref.shape[2])
 
     chunks = c_rsem.shape[0]
-    width = D // chunks
+    ends = (0, D // 4, D // 2, 3 * D // 4, D)
+    z_chunks = zf_rsem.shape[0]
+    half = ends[z_chunks]
+
+    def late(i):
+        return slice(ends[i] - half, ends[i + 1] - half)
 
     def cut(i):
-        return slice(i * width, (i + 1) * width)
+        return slice(ends[i], ends[i + 1])
 
     def core_copy(i):
         return remote(
@@ -676,51 +704,108 @@
 
     def row_copy(i):
         return remote(
-            y_send.at[:, old_rows, cut(i)],
-            y_recv.at[:, old_rows, cut(i)],
+            y_send.at[:, old_rows, late(i)],
+            y_recv.at[:, old_rows, late(i)],
             y_ssem,
-            y_rsem.at[i],
+            y_rsem.at[i - z_chunks],
             other_row,
         )
 
     def line_copy(i, k):
         to = lax.rem(line + k, lines)
         return remote(
-            z_send.at[k, old_rows, cut(i)],
-            z_recv.at[k, old_rows, cut(i)],
+            z_send.at[k, old_rows, late(i)],
+            z_recv.at[k, old_rows, late(i)],
             z_sem.at[0],
             z_sem.at[1],
             device(to, row, core),
         )
 
-    activated = activate(x_a, gates_a)
-    for i in range(chunks):
-        rows = jnp.dot(activated, w_down[:, cut(i)], preferred_element_type=f32)
-        part_a[:, :, :, :, cut(i)] = rows.astype(bf16).reshape(2, 2, lines, seqs, width)
-        core_copy(i).start()
-
-    for pool in b_pools:
-        b_spots(pool, chips - 1, 0).wait_recv()
-        b_spots(pool, chips, 1).start()
-
-    for i in range(chunks):
+    for n in range(3):
+        for pool in pools:
+            y_arrive(pool, n)
+    for pool in pools:
+        pass_on(pool, (1 - core) * chips, chips, at_core, other_core).wait_recv()
+    activated = activate(rows_of(x_a), rows_of(gates_a))
+
+    def zf_copy(i, k):
+        to = lax.rem(line + k, lines)
+        return remote(
+            zf_send.at[k, :, old_rows, cut(i)],
+            zf_recv.at[k, :, old_rows, cut(i)],
+            zf_ssem,
+            zf_rsem.at[i],
+            device(to, row, core),
+        )
+
+    def held_by(at_row, at_line, i):
+        return part_a[core, at_row, at_line, :, cut(i)].astype(f32) + core_a[
+            at_row, at_line, :, cut(i)
+        ].astype(f32)
+
+    def zf_step(i):
         core_copy(i).wait_recv()
-        y_send[:, :, cut(i)] = (
+        for k in (2, 1, 3):
+            for at_row in range(2):
+                zf_send[k, at_row, :, cut(i)] = held_by(
+                    at_row, lax.rem(line + k, lines), i
+                ).astype(bf16)
+            zf_copy(i, k).start()
+
+    def yf_copy():
+        return remote(
+            yf_send.at[old_rows], yf_recv.at[old_rows], yf_sem.at[0], yf_sem.at[1], other_row
+        )
+
+    def yf_step(i):
+        ref = zf_recv.at[pl.ds(1, lines - 1), :, old_rows, cut(i)]
+        remote(ref, ref, zf_ssem, zf_rsem.at[i], other_core).wait_recv()
+
+        def summed(at_row):
+            total = held_by(at_row, line, i)
+            for k in range(1, lines):
+                total = total + zf_recv[k, at_row, :, cut(i)].astype(f32)
+            return total
+
+        yf_send[:, cut(i)] = summed(1 - row).astype(bf16)
+        kept[:, cut(i)] = attn[:, cut(i)] + summed(row)
+
+    def row_step(i):
+        if i < z_chunks:
+            zf_step(i)
+            return
+        core_copy(i).wait_recv()
+        y_send[:, :, late(i)] = (
             part_a[core, 1 - row, :, :, cut(i)].astype(f32)
             + core_a[1 - row, :, :, cut(i)].astype(f32)
         ).astype(bf16)
         row_copy(i).start()
 
+    behind = 3
+    for i in range(chunks):
+        rows = jnp.dot(activated, w_down[:, cut(i)], preferred_element_type=f32)
+        part_a[:, :, :, :, cut(i)] = rows.astype(bf16).reshape(
+            2, 2, lines, seqs, ends[i + 1] - ends[i]
+        )
+        core_copy(i).start()
+        if i == 1:
+            for pool in b_pools:
+                b_pass(pool)
+        if i >= behind:
+            row_step(i - behind)
+    for i in range(chunks - behind, chunks):
+        row_step(i)
+
     for pool in b_pools:
-        b_spots(pool, chips, 1).wait_recv()
-    activated = activate(x_b, gates_b)
+        b_core_copy(pool, 0, chips).wait_recv()
+    activated = activate(rows_of(x_b), rows_of(gates_b))
     b_chunks = cb_rsem.shape[0]
     b_width = D // b_chunks
 
     def b_core(i):
         at = slice(i * b_width, (i + 1) * b_width)
         return remote(
-            part_b.at[1 - core, :, new_rows, at],
+            part_b.at[core, :, new_rows, at],
             core_b.at[:, new_rows, at],
             cb_ssem,
             cb_rsem.at[i],
@@ -739,50 +824,60 @@
             recv_b.at[unit, new_rows],
             rb_sem.at[0],
             rb_sem.at[1],
-            device_of(to, core),
-        )
-
-    for i in range(chunks):
+            device_of(to, 1 - core),
+        )
+
+    def line_step(i):
         row_copy(i).wait_recv()
 
         def summed(at_line):
             return (
                 part_a[core, row, at_line, :, cut(i)].astype(f32)
                 + core_a[row, at_line, :, cut(i)].astype(f32)
-                + y_recv[at_line, :, cut(i)].astype(f32)
+                + y_recv[at_line, :, late(i)].astype(f32)
             )
 
         for k in range(1, lines):
-            z_send[k, :, cut(i)] = summed(lax.rem(line + k, lines)).astype(bf16)
+            z_send[k, :, late(i)] = summed(lax.rem(line + k, lines)).astype(bf16)
             line_copy(i, k).start()
         kept[:, cut(i)] = attn[:, cut(i)] + summed(line)
 
+    early = chunks - 1
+    for i in range(z_chunks, early):
+        line_step(i)
     for i in range(b_chunks):
         b_core(i).wait_recv()
-    for to in other_units():
-        sum_b[to] = (part_b[core, to].astype(f32) + core_b[to].astype(f32)).astype(bf16)
+    for to in all_units():
+        sum_b[to] = (part_b[1 - core, to].astype(f32) + core_b[to].astype(f32)).astype(bf16)
         b_return(to).start()
-    last = attn[...] + part_b[core, unit].astype(f32) + core_b[unit].astype(f32)
+    for i in range(early, chunks):
+        line_step(i)
+    for i in range(z_chunks):
+        yf_step(i)
+    yf_copy().start()
 
     rest = pl.ds(1, lines - 1)
     z_all = remote(
         z_recv.at[rest, old_rows], z_recv.at[rest, old_rows], z_sem.at[0], z_sem.at[1], other_core
     )
     z_all.wait_recv()
-    answer = kept[...]
+    answer = kept[:, half:]
     for k in range(1, lines):
         answer = answer + z_recv[k].astype(f32)
+    yf_copy().wait_recv()
+    answer = jnp.concatenate([kept[:, :half] + yf_recv[...].astype(f32), answer], 1)
 
     b_all = remote(
-        recv_b.at[few, new_rows], recv_b.at[few, new_rows], rb_sem.at[0], rb_sem.at[1], other_core
+        recv_b.at[:, new_rows], recv_b.at[:, new_rows], rb_sem.at[0], rb_sem.at[1], other_core
     )
     b_all.wait_recv()
-    for k in range(1, chips):
-        last = last + recv_b[lax.rem(unit + k, chips)].astype(f32)
+    last = attn[...]
+    for u in range(chips):
+        last = last + recv_b[u].astype(f32)
     is_b = lax.broadcasted_iota(jnp.int32, (seqs, D), 0) < MAXP
     out_ref[...] = jnp.where(is_b, last, answer).astype(bf16)
 
-    for copy in (page_copy, q_all, z_all, b_all) + o_all:
+    for copy in (page_copy, q_all, z_all, b_all, yf_copy()) + o_all:
         copy.wait_send()
     for n, (buffer, rows) in enumerate(((x_a, old_rows), (gates_a, pl.ds(0, seqs)))):
         ref = buffer.at[pl.ds(0, 4 * lines - 1), rows]
@@ -793,6 +888,7 @@
     for ref, ssem, rsem in (
         (part_a.at[0, :, :, old_rows], c_ssem, c_rsem.at[0]),
         (y_send.at[:, old_rows], y_ssem, y_rsem.at[0]),
+        (zf_send.at[pl.ds(1, lines - 1), :, old_rows], zf_ssem, zf_rsem.at[0]),
         (part_b.at[0, :, new_rows], cb_ssem, cb_rsem.at[0]),
     ):
         remote(ref, ref, ssem, rsem, other_core).wait_send()
@@ -821,7 +917,7 @@
     lines = devices // 4
     chips = devices // 2
     bf16, f32 = jnp.bfloat16, jnp.float32
-    chunks = 4
+    chunks, z_chunks = 4, 2
     b_chunks = 2
     packed = D * MAXP // seqs
     loaded = (
@@ -862,10 +958,14 @@
             pltpu.VMEM((devices, seqs, 128), f32),
             pltpu.VMEM((2, 2, lines, seqs, D), bf16),
             pltpu.VMEM((2, lines, seqs, D), bf16),
-            pltpu.VMEM((lines, seqs, D), bf16),
-            pltpu.VMEM((lines, seqs, D), bf16),
-            pltpu.VMEM((lines, seqs, D), bf16),
-            pltpu.VMEM((lines, seqs, D), bf16),
+            pltpu.VMEM((lines, seqs, D // 2), bf16),
+            pltpu.VMEM((lines, seqs, D // 2), bf16),
+            pltpu.VMEM((lines, seqs, D // 2), bf16),
+            pltpu.VMEM((lines, seqs, D // 2), bf16),
+            pltpu.VMEM((lines, 2, seqs, D // 2), bf16),
+            pltpu.VMEM((lines, 2, seqs, D // 2), bf16),
+            pltpu.VMEM((seqs, D // 2), bf16),
+            pltpu.VMEM((seqs, D // 2), bf16),
             pltpu.VMEM((seqs, D), f32),
             pltpu.VMEM((2, chips, seqs, D), bf16),
             pltpu.VMEM((chips, seqs, D), bf16),
@@ -878,13 +978,16 @@
             dma((2,)),
             dma((2,)),
             dma((2,)),
-            dma((2, lines + 2)),
+            dma((2, 2 * lines)),
             dma((2,)),
             dma((2, 2)),
             dma(()),
             dma((chunks,)),
             dma(()),
-            dma((chunks,)),
+            dma((chunks - z_chunks,)),
+            dma((2,)),
+            dma(()),
+            dma((z_chunks,)),
             dma((2,)),
             dma(()),
             dma((b_chunks,)),

time: 39.1 us -> 37 us (0.946)
  Pallas kernels: 38.3 us -> 36.2 us
    pallas_call x1, Pallas kernels: 38.3 us -> 36.2 us  [dense(): pl.pallas_call(functools.partial(layer_kernel, devices), out_shape=pltpu....]
where the time goes in v3:
time: 37 us; the launch traced here: 36.8 us
  Pallas kernels  36.2 us (98%)
  local copies, waits for them, and re-layouts  0.63 us (2%)
    pallas_call x1, Pallas kernels, dense(): pl.pallas_call(functools.partial(layer_kernel, devices), out_shape=pltpu....  36.2 us

profile of v3, /device:TPU:0, one launch (start us, length us, event | category | flops | bytes accessed | tf_op | source)
XLA Modules:
  0.0 36.8 jit_solution(4734333623120978792)
XLA Ops:
  0.0 36.2 %shard_map.145 = bf16[8,4096]{1,0:T(8,128)(2,1)S(1)} custom-call(s32[16]{0:T(128)} %owners_hbm.1, s32[16]{0:T(128)} %lengths_hbm.1, s32[8]{0:T(128)} %blocks_hbm.1, bf16[16,2,16,256]{3,2,1,0:T(8,128)(2,1)} %bitcast.3, bf16[8,4096]{1,0:T(8,128)(2,1)} %q_hbm.1, bf16[8,2,256]{2,1,0:T(2,128)(2,1)} %dkv_hbm.1, s32[8,16]{1,0:T(8,128)} %table_hbm.1, ...), custom_call_target="tpu_custom_call" | custom-call | tf_op jit(solution)/shard_map/pallas_call | solution.py:937
  36.2 0.6 %copy.17 = bf16[8,4096]{1,0:T(8,128)(2,1)} copy(bf16[8,4096]{1,0:T(8,128)(2,1)S(1)} %shard_map.145) | data formatting | bytes 131072

commit v4 on v3

--- a/solution.py
+++ b/solution.py
@@ -228,7 +228,6 @@
     lse_recv,
     attn,
     x_a,
-    gates_a,
     x_b,
     gates_b,
     part_a,
@@ -464,7 +463,7 @@
         return jnp.concatenate([gate] * (128 // experts), 1)
 
     normed = norm_of(residual_of(attn[...]))
-    x_a[mine] = normed
+    x_a[mine, :, :D] = normed
     pl.semaphore_wait(barrier, devices - 1)
 
     def q_copy(to):
@@ -478,8 +477,8 @@
 
 
     def pass_on(pool, spot, count, at, to):
-        buffer, rows, n = pool
-        ref = buffer.at[pl.ds(spot, count), rows]
+        buffer, rows, cols, n = pool
+        ref = buffer.at[pl.ds(spot, count), rows, cols]
         return remote(ref, ref, xa_ssem.at[n], xa_rsem.at[n, at], to)
 
     far, near = lax.rem(line + 2, lines), line + 1 - 2 * lax.rem(line, 2)
@@ -513,10 +512,20 @@
         pass_on(pool, mine, 1, at_near, near_device).start()
         cross(pool, mine, 3)
 
-    pools = [(x_a, old_rows, 0), (gates_a, pl.ds(0, seqs), 1)]
-    first_hops(pools[0])
-    gates_a[mine] = gate_of(normed)
-    first_hops(pools[1])
+    pieces = xa_ssem.shape[0]
+    piece = D // pieces
+    sizes = [piece] * (pieces - 1) + [piece + 128]
+    pools = [(x_a, old_rows, pl.ds(n * piece, sizes[n]), n) for n in range(pieces)]
+    for pool in pools[:-1]:
+        first_hops(pool)
+    gate = gate_of(normed)
+    high = gate.astype(bf16)
+    x_a[mine, :, D:] = jnp.where(
+        lax.broadcasted_iota(jnp.int32, (seqs, 128), 1) < 128 // 2,
+        high.astype(f32),
+        gate - high.astype(f32),
+    ).astype(bf16)
+    first_hops(pools[-1])
 
     prompts = owners.shape[0]
     shape = (1, prompts * PAGE_TOKENS)
@@ -543,6 +552,22 @@
 
     q_all = remote(q_recv, q_recv, q_sem.at[0], q_sem.at[1], other_core)
     q_all.wait_recv()
+    wide_kv = per_kv * HEAD_SIZE
+
+    def o_copy(to, h):
+        cols = pl.ds(h * wide_kv, wide_kv)
+        return remote(
+            o_send.at[to, :, cols],
+            o_recv.at[unit, :, cols],
+            o_sem.at[0],
+            o_sem.at[1],
+            device_of(to, 1 - core),
+        )
+
+    def lse_copy(to):
+        at = device_of(to, 1 - core)
+        return remote(lse_send.at[to], lse_recv.at[unit], lse_sem.at[0], lse_sem.at[1], at)
+
     lane_of = lax.broadcasted_iota(jnp.int32, (slots, 128), 1)
     lse_all = jnp.zeros((slots, 128), f32)
     for h in range(KEY_VALUE_HEADS):
@@ -571,18 +596,12 @@
             rows = slice(j * slots, (j + 1) * slots)
             o_send[:, :, head_cols(hh)] = mixed[rows].astype(bf16).reshape(chips, seqs, HEAD_SIZE)
             lse_all = jnp.where(lane_of == hh, lse[rows], lse_all)
+        for to in all_units():
+            o_copy(to, h).start()
     lse_send[...] = lse_all.reshape(chips, seqs, 128)
 
-    def o_copy(to):
-        at = device_of(to, 1 - core)
-        return (
-            remote(o_send.at[to], o_recv.at[unit], o_sem.at[0], o_sem.at[1], at),
-            remote(lse_send.at[to], lse_recv.at[unit], lse_sem.at[0], lse_sem.at[1], at),
-        )
-
     for to in all_units():
-        for copy in o_copy(to):
-            copy.start()
+        lse_copy(to).start()
 
     for pool in pools:
         z_arrive(pool, at_far)
@@ -669,12 +688,13 @@
     for copy in weights:
         copy.wait()
 
-    def activate(x, gate):
-        total = x.shape[0]
+    def activate(both, gate, parts):
         lanes_of = lax.broadcasted_iota(jnp.int32, (total, 128), 1)
-        both = jnp.dot(x, w_in[...], preferred_element_type=f32)
         gate_proj, up_proj = both[:, :hidden], both[:, hidden:]
-        scaled = jnp.sum(jnp.where(lanes_of == me // 2, gate, 0.0), -1, keepdims=True)
+        kept_lanes = lanes_of == me // 2
+        if parts == 2:
+            kept_lanes = kept_lanes | (lanes_of == 128 // 2 + me // 2)
+        scaled = jnp.sum(jnp.where(kept_lanes, gate, 0.0), -1, keepdims=True)
         return (gate_proj / (1.0 + jnp.exp(-gate_proj)) * up_proj * scaled).astype(bf16)
 
     total = devices * seqs
@@ -721,12 +741,22 @@
             device(to, row, core),
         )
 
-    for n in range(3):
+    for n in range(2):
         for pool in pools:
             y_arrive(pool, n)
     for pool in pools:
+        y_arrive(pool, 2)
+
+    def core_arrive(pool):
         pass_on(pool, (1 - core) * chips, chips, at_core, other_core).wait_recv()
-    activated = activate(rows_of(x_a), rows_of(gates_a))
+
+    both = jnp.zeros((total, 2 * hidden), f32)
+    for n in range(pieces):
+        core_arrive(pools[n])
+        cols = slice(n * piece, (n + 1) * piece)
+        x = x_a[:, :, cols].reshape(total, piece)
+        both = both + jnp.dot(x, w_in[cols], preferred_element_type=f32)
+    activated = activate(both, x_a[:, :, D:].reshape(total, 128).astype(f32), 2)
 
     def zf_copy(i, k):
         to = lax.rem(line + k, lines)
@@ -781,7 +811,7 @@
         ).astype(bf16)
         row_copy(i).start()
 
-    behind = 3
+    behind = 2
     for i in range(chunks):
         rows = jnp.dot(activated, w_down[:, cut(i)], preferred_element_type=f32)
         part_a[:, :, :, :, cut(i)] = rows.astype(bf16).reshape(
@@ -798,7 +828,8 @@
 
     for pool in b_pools:
         b_core_copy(pool, 0, chips).wait_recv()
-    activated = activate(rows_of(x_b), rows_of(gates_b))
+    both = jnp.dot(rows_of(x_b), w_in[...], preferred_element_type=f32)
+    activated = activate(both, rows_of(gates_b), 1)
     b_chunks = cb_rsem.shape[0]
     b_width = D // b_chunks
 
@@ -879,9 +910,8 @@
 
     for copy in (page_copy, q_all, z_all, b_all, yf_copy()) + o_all:
         copy.wait_send()
-    for n, (buffer, rows) in enumerate(((x_a, old_rows), (gates_a, pl.ds(0, seqs)))):
-        ref = buffer.at[pl.ds(0, 4 * lines - 1), rows]
-        remote(ref, ref, xa_ssem.at[n], xa_rsem.at[n, 0], other_core).wait_send()
+    for pool in pools:
+        pass_on(pool, 0, 4 * lines - 1, 0, other_core).wait_send()
     for n, (buffer, rows) in enumerate(((x_b, new_rows), (gates_b, pl.ds(0, seqs)))):
         ref = buffer.at[pl.ds(0, 2 * chips - 1), rows]
         remote(ref, ref, xb_ssem.at[n], xb_rsem.at[n, 0], other_core).wait_send()
@@ -918,6 +948,7 @@
     chips = devices // 2
     bf16, f32 = jnp.bfloat16, jnp.float32
     chunks, z_chunks = 4, 2
+    pieces = 2
     b_chunks = 2
     packed = D * MAXP // seqs
     loaded = (
@@ -952,8 +983,7 @@
             pltpu.VMEM((chips, seqs, 128), f32),
             pltpu.VMEM((chips, seqs, 128), f32),
             pltpu.VMEM((seqs, D), f32),
-            pltpu.VMEM((devices, seqs, D), bf16),
-            pltpu.VMEM((devices, seqs, 128), f32),
+            pltpu.VMEM((devices, seqs, D + 128), bf16),
             pltpu.VMEM((devices, seqs, D), bf16),
             pltpu.VMEM((devices, seqs, 128), f32),
             pltpu.VMEM((2, 2, lines, seqs, D), bf16),
@@ -977,8 +1007,8 @@
             dma((2,)),
             dma((2,)),
             dma((2,)),
-            dma((2,)),
-            dma((2, 2 * lines)),
+            dma((pieces,)),
+            dma((pieces, 2 * lines)),
             dma((2,)),
             dma((2, 2)),
             dma(()),

time: 37 us -> 36.1 us (0.976)
  Pallas kernels: 36.2 us -> 35.3 us
    pallas_call x1, Pallas kernels: 36.2 us -> 35.3 us  [dense(): pl.pallas_call(functools.partial(layer_kernel, devices), out_shape=pltpu....]
where the time goes in v4:
time: 36.1 us; the launch traced here: 35.9 us
  Pallas kernels  35.3 us (98%)
  local copies, waits for them, and re-layouts  0.63 us (2%)
    pallas_call x1, Pallas kernels, dense(): pl.pallas_call(functools.partial(layer_kernel, devices), out_shape=pltpu....  35.3 us

profile of v4, /device:TPU:0, one launch (start us, length us, event | category | flops | bytes accessed | tf_op | source)
XLA Modules:
  0.0 35.9 jit_solution(15752783516301258422)
XLA Ops:
  0.0 35.3 %shard_map.145 = bf16[8,4096]{1,0:T(8,128)(2,1)S(1)} custom-call(s32[16]{0:T(128)} %owners_hbm.1, s32[16]{0:T(128)} %lengths_hbm.1, s32[8]{0:T(128)} %blocks_hbm.1, bf16[16,2,16,256]{3,2,1,0:T(8,128)(2,1)} %bitcast.3, bf16[8,4096]{1,0:T(8,128)(2,1)} %q_hbm.1, bf16[8,2,256]{2,1,0:T(2,128)(2,1)} %dkv_hbm.1, s32[8,16]{1,0:T(8,128)} %table_hbm.1, ...), custom_call_target="tpu_custom_call" | custom-call | tf_op jit(solution)/shard_map/pallas_call | solution.py:968
  35.3 0.6 %copy.17 = bf16[8,4096]{1,0:T(8,128)(2,1)} copy(bf16[8,4096]{1,0:T(8,128)(2,1)S(1)} %shard_map.145) | data formatting | bytes 131072

commit v5 on v4

--- a/solution.py
+++ b/solution.py
@@ -232,14 +232,10 @@
     gates_b,
     part_a,
     core_a,
+    z_send,
+    z_recv,
     y_send,
     y_recv,
-    z_send,
-    z_recv,
-    zf_send,
-    zf_recv,
-    yf_send,
-    yf_recv,
     kept,
     part_b,
     core_b,
@@ -257,12 +253,10 @@
     xb_rsem,
     c_ssem,
     c_rsem,
+    z_ssem,
+    z_rsem,
     y_ssem,
     y_rsem,
-    z_sem,
-    zf_ssem,
-    zf_rsem,
-    yf_sem,
     cb_ssem,
     cb_rsem,
     rb_sem,
@@ -484,7 +478,7 @@
     far, near = lax.rem(line + 2, lines), line + 1 - 2 * lax.rem(line, 2)
     far_device, near_device = device(far, row, 1 - core), device(near, row, 1 - core)
     row_device = device(line, 1 - row, 1 - core)
-    at_far, at_near, at_relay, at_core = 0, 1, 2, 7
+    at_far, at_near, at_relay, at_core = 0, 1, 2, (7, 8)
     sources = (far, near, lax.rem(near + 2, lines), line)
     z_cores, y_cores = (1 - core, 1 - core, core), (core, core, 1 - core, 1 - core)
 
@@ -493,7 +487,7 @@
 
     def cross(pool, spot, n):
         pass_on(pool, spot, 1, at_y(n), row_device).start()
-        pass_on(pool, spot, 1, at_core, other_core).start()
+        pass_on(pool, spot, 1, at_core[0], other_core).start()
 
     def z_arrive(pool, n):
         spot = place(sources[n], row, z_cores[n])
@@ -505,7 +499,7 @@
     def y_arrive(pool, n):
         spot = place(sources[n], 1 - row, y_cores[n])
         pass_on(pool, spot, 1, at_y(n), other_row).wait_recv()
-        pass_on(pool, spot, 1, at_core, other_core).start()
+        pass_on(pool, spot, 1, at_core[1], other_core).start()
 
     def first_hops(pool):
         pass_on(pool, mine, 1, at_far, far_device).start()
@@ -689,7 +683,7 @@
         copy.wait()
 
     def activate(both, gate, parts):
-        lanes_of = lax.broadcasted_iota(jnp.int32, (total, 128), 1)
+        lanes_of = lax.broadcasted_iota(jnp.int32, gate.shape, 1)
         gate_proj, up_proj = both[:, :hidden], both[:, hidden:]
         kept_lanes = lanes_of == me // 2
         if parts == 2:
@@ -702,70 +696,59 @@
     def rows_of(ref):
         return ref[...].reshape(total, ref.shape[2])
 
-    chunks = c_rsem.shape[0]
+    chunks = c_rsem.shape[1]
     ends = (0, D // 4, D // 2, 3 * D // 4, D)
-    z_chunks = zf_rsem.shape[0]
-    half = ends[z_chunks]
-
-    def late(i):
-        return slice(ends[i] - half, ends[i + 1] - half)
 
     def cut(i):
         return slice(ends[i], ends[i + 1])
 
-    def core_copy(i):
+    def core_copy(n, i):
         return remote(
-            part_a.at[1 - core, :, :, old_rows, cut(i)],
-            core_a.at[:, :, old_rows, cut(i)],
+            part_a.at[1 - core, kinds[n], :, old_rows, cut(i)],
+            core_a.at[kinds[n], :, old_rows, cut(i)],
             c_ssem,
-            c_rsem.at[i],
+            c_rsem.at[n, i],
             other_core,
-        )
-
-    def row_copy(i):
-        return remote(
-            y_send.at[:, old_rows, late(i)],
-            y_recv.at[:, old_rows, late(i)],
-            y_ssem,
-            y_rsem.at[i - z_chunks],
-            other_row,
-        )
-
-    def line_copy(i, k):
-        to = lax.rem(line + k, lines)
-        return remote(
-            z_send.at[k, old_rows, late(i)],
-            z_recv.at[k, old_rows, late(i)],
-            z_sem.at[0],
-            z_sem.at[1],
-            device(to, row, core),
         )
 
     for n in range(2):
         for pool in pools:
             y_arrive(pool, n)
-    for pool in pools:
-        y_arrive(pool, 2)
-
-    def core_arrive(pool):
-        pass_on(pool, (1 - core) * chips, chips, at_core, other_core).wait_recv()
-
-    both = jnp.zeros((total, 2 * hidden), f32)
-    for n in range(pieces):
-        core_arrive(pools[n])
-        cols = slice(n * piece, (n + 1) * piece)
-        x = x_a[:, :, cols].reshape(total, piece)
-        both = both + jnp.dot(x, w_in[cols], preferred_element_type=f32)
-    activated = activate(both, x_a[:, :, D:].reshape(total, 128).astype(f32), 2)
-
-    def zf_copy(i, k):
+
+    def core_arrive(n):
+        for pool in pools:
+            pass_on(pool, 0, lines, at_core[n], other_core).wait_recv()
+
+    def row_activated(at_row):
+        x = jnp.concatenate(
+            [
+                x_a[pl.ds((at * 2 + at_row) * lines, lines)].reshape(lines * seqs, D + 128)
+                for at in range(2)
+            ],
+            0,
+        )
+        both = jnp.dot(x[:, :D], w_in[...], preferred_element_type=f32)
+        return activate(both, x[:, D:].astype(f32), 2)
+
+    kinds = (row, 1 - row)
+
+    def z_sum_copy(n, i, k):
         to = lax.rem(line + k, lines)
         return remote(
-            zf_send.at[k, :, old_rows, cut(i)],
-            zf_recv.at[k, :, old_rows, cut(i)],
-            zf_ssem,
-            zf_rsem.at[i],
+            z_send.at[k, kinds[n], old_rows, cut(i)],
+            z_recv.at[k, kinds[n], old_rows, cut(i)],
+            z_ssem,
+            z_rsem.at[n, i],
             device(to, row, core),
+        )
+
+    def y_sum_copy(i):
+        return remote(
+            y_send.at[old_rows, cut(i)],
+            y_recv.at[old_rows, cut(i)],
+            y_ssem,
+            y_rsem.at[i],
+            other_row,
         )
 
     def held_by(at_row, at_line, i):
@@ -773,58 +756,63 @@
             at_row, at_line, :, cut(i)
         ].astype(f32)
 
-    def zf_step(i):
-        core_copy(i).wait_recv()
+    def z_step(n, i):
+        core_copy(n, i).wait_recv()
         for k in (2, 1, 3):
-            for at_row in range(2):
-                zf_send[k, at_row, :, cut(i)] = held_by(
-                    at_row, lax.rem(line + k, lines), i
-                ).astype(bf16)
-            zf_copy(i, k).start()
-
-    def yf_copy():
-        return remote(
-            yf_send.at[old_rows], yf_recv.at[old_rows], yf_sem.at[0], yf_sem.at[1], other_row
-        )
-
-    def yf_step(i):
-        ref = zf_recv.at[pl.ds(1, lines - 1), :, old_rows, cut(i)]
-        remote(ref, ref, zf_ssem, zf_rsem.at[i], other_core).wait_recv()
+            z_send[k, kinds[n], :, cut(i)] = held_by(
+                kinds[n], lax.rem(line + k, lines), i
+            ).astype(bf16)
+            z_sum_copy(n, i, k).start()
+
+    def y_step(i):
+        for n in range(2):
+            ref = z_recv.at[pl.ds(1, lines - 1), kinds[n], old_rows, cut(i)]
+            remote(ref, ref, z_ssem, z_rsem.at[n, i], other_core).wait_recv()
 
         def summed(at_row):
-            total = held_by(at_row, line, i)
+            value = held_by(at_row, line, i)
             for k in range(1, lines):
-                total = total + zf_recv[k, at_row, :, cut(i)].astype(f32)
-            return total
-
-        yf_send[:, cut(i)] = summed(1 - row).astype(bf16)
+                value = value + z_recv[k, at_row, :, cut(i)].astype(f32)
+            return value
+
+        y_send[:, cut(i)] = summed(1 - row).astype(bf16)
+        y_sum_copy(i).start()
         kept[:, cut(i)] = attn[:, cut(i)] + summed(row)
 
-    def row_step(i):
-        if i < z_chunks:
-            zf_step(i)
-            return
-        core_copy(i).wait_recv()
-        y_send[:, :, late(i)] = (
-            part_a[core, 1 - row, :, :, cut(i)].astype(f32)
-            + core_a[1 - row, :, :, cut(i)].astype(f32)
-        ).astype(bf16)
-        row_copy(i).start()
+    def down(n, i, activated):
+        rows = jnp.dot(activated, w_down[:, cut(i)], preferred_element_type=f32)
+        part_a[:, kinds[n], :, :, cut(i)] = rows.astype(bf16).reshape(
+            2, lines, seqs, ends[i + 1] - ends[i]
+        )
+        core_copy(n, i).start()
+
+    def expert_rows(n, between):
+        core_arrive(n)
+        activated = row_activated(kinds[n])
+        between[0]()
+        for i in range(chunks):
+            down(n, i, activated)
+            if i == 1:
+                between[1]()
+            if i >= behind:
+                z_step(n, i - behind)
+        for i in range(chunks - behind, chunks):
+            z_step(n, i)
+
+    def finish_gather():
+        for pool in pools:
+            y_arrive(pool, 2)
+
+    def pass_b():
+        for pool in b_pools:
+            b_pass(pool)
+
+    def nothing():
+        pass
 
     behind = 2
-    for i in range(chunks):
-        rows = jnp.dot(activated, w_down[:, cut(i)], preferred_element_type=f32)
-        part_a[:, :, :, :, cut(i)] = rows.astype(bf16).reshape(
-            2, 2, lines, seqs, ends[i + 1] - ends[i]
-        )
-        core_copy(i).start()
-        if i == 1:
-            for pool in b_pools:
-                b_pass(pool)
-        if i >= behind:
-            row_step(i - behind)
-    for i in range(chunks - behind, chunks):
-        row_step(i)
+    expert_rows(0, (finish_gather, nothing))
+    expert_rows(1, (nothing, pass_b))
 
     for pool in b_pools:
         b_core_copy(pool, 0, chips).wait_recv()
@@ -858,46 +846,13 @@
             device_of(to, 1 - core),
         )
 
-    def line_step(i):
-        row_copy(i).wait_recv()
-
-        def summed(at_line):
-            return (
-                part_a[core, row, at_line, :, cut(i)].astype(f32)
-                + core_a[row, at_line, :, cut(i)].astype(f32)
-                + y_recv[at_line, :, late(i)].astype(f32)
-            )
-
-        for k in range(1, lines):
-            z_send[k, :, late(i)] = summed(lax.rem(line + k, lines)).astype(bf16)
-            line_copy(i, k).start()
-        kept[:, cut(i)] = attn[:, cut(i)] + summed(line)
-
-    early = chunks - 1
-    for i in range(z_chunks, early):
-        line_step(i)
     for i in range(b_chunks):
         b_core(i).wait_recv()
     for to in all_units():
         sum_b[to] = (part_b[1 - core, to].astype(f32) + core_b[to].astype(f32)).astype(bf16)
         b_return(to).start()
-    for i in range(early, chunks):
-        line_step(i)
-    for i in range(z_chunks):
-        yf_step(i)
-    yf_copy().start()
-
-    rest = pl.ds(1, lines - 1)
-    z_all = remote(
-        z_recv.at[rest, old_rows], z_recv.at[rest, old_rows], z_sem.at[0], z_sem.at[1], other_core
-    )
-    z_all.wait_recv()
-    answer = kept[:, half:]
-    for k in range(1, lines):
-        answer = answer + z_recv[k].astype(f32)
-    yf_copy().wait_recv()
-    answer = jnp.concatenate([kept[:, :half] + yf_recv[...].astype(f32), answer], 1)
-
+    for i in range(chunks):
+        y_step(i)
     b_all = remote(
         recv_b.at[:, new_rows], recv_b.at[:, new_rows], rb_sem.at[0], rb_sem.at[1], other_core
     )
@@ -905,10 +860,13 @@
     last = attn[...]
     for u in range(chips):
         last = last + recv_b[u].astype(f32)
+    for i in range(chunks):
+        y_sum_copy(i).wait_recv()
+    answer = kept[...] + y_recv[...].astype(f32)
     is_b = lax.broadcasted_iota(jnp.int32, (seqs, D), 0) < MAXP
     out_ref[...] = jnp.where(is_b, last, answer).astype(bf16)
 
-    for copy in (page_copy, q_all, z_all, b_all, yf_copy()) + o_all:
+    for copy in (page_copy, q_all, b_all) + o_all:
         copy.wait_send()
     for pool in pools:
         pass_on(pool, 0, 4 * lines - 1, 0, other_core).wait_send()
@@ -916,9 +874,9 @@
         ref = buffer.at[pl.ds(0, 2 * chips - 1), rows]
         remote(ref, ref, xb_ssem.at[n], xb_rsem.at[n, 0], other_core).wait_send()
     for ref, ssem, rsem in (
-        (part_a.at[0, :, :, old_rows], c_ssem, c_rsem.at[0]),
-        (y_send.at[:, old_rows], y_ssem, y_rsem.at[0]),
-        (zf_send.at[pl.ds(1, lines - 1), :, old_rows], zf_ssem, zf_rsem.at[0]),
+        (part_a.at[0, :, :, old_rows], c_ssem, c_rsem.at[0, 0]),
+        (z_send.at[pl.ds(1, lines - 1), :, old_rows], z_ssem, z_rsem.at[0, 0]),
+        (y_send.at[old_rows], y_ssem, y_rsem.at[0]),
         (part_b.at[0, :, new_rows], cb_ssem, cb_rsem.at[0]),
     ):
         remote(ref, ref, ssem, rsem, other_core).wait_send()
@@ -947,7 +905,7 @@
     lines = devices // 4
     chips = devices // 2
     bf16, f32 = jnp.bfloat16, jnp.float32
-    chunks, z_chunks = 4, 2
+    chunks = 4
     pieces = 2
     b_chunks = 2
     packed = D * MAXP // seqs
@@ -988,14 +946,10 @@
             pltpu.VMEM((devices, seqs, 128), f32),
             pltpu.VMEM((2, 2, lines, seqs, D), bf16),
             pltpu.VMEM((2, lines, seqs, D), bf16),
-            pltpu.VMEM((lines, seqs, D // 2), bf16),
-            pltpu.VMEM((lines, seqs, D // 2), bf16),
-            pltpu.VMEM((lines, seqs, D // 2), bf16),
-            pltpu.VMEM((lines, seqs, D // 2), bf16),
-            pltpu.VMEM((lines, 2, seqs, D // 2), bf16),
-            pltpu.VMEM((lines, 2, seqs, D // 2), bf16),
-            pltpu.VMEM((seqs, D // 2), bf16),
-            pltpu.VMEM((seqs, D // 2), bf16),
+            pltpu.VMEM((lines, 2, seqs, D), bf16),
+            pltpu.VMEM((lines, 2, seqs, D), bf16),
+            pltpu.VMEM((seqs, D), bf16),
+            pltpu.VMEM((seqs, D), bf16),
             pltpu.VMEM((seqs, D), f32),
             pltpu.VMEM((2, chips, seqs, D), bf16),
             pltpu.VMEM((chips, seqs, D), bf16),
@@ -1008,17 +962,15 @@
             dma((2,)),
             dma((2,)),
             dma((pieces,)),
-            dma((pieces, 2 * lines)),
+            dma((pieces, 2 * lines + 1)),
             dma((2,)),
             dma((2, 2)),
             dma(()),
+            dma((2, chunks)),
+            dma(()),
+            dma((2, chunks)),
+            dma(()),
             dma((chunks,)),
-            dma(()),
-            dma((chunks - z_chunks,)),
-            dma((2,)),
-            dma(()),
-            dma((z_chunks,)),
-            dma((2,)),
             dma(()),
             dma((b_chunks,)),
             dma((2,)),

time: 36.1 us -> 35.4 us (0.981)
  Pallas kernels: 35.3 us -> 34.7 us
    pallas_call x1, Pallas kernels: 35.3 us -> 34.7 us  [dense(): pl.pallas_call(functools.partial(layer_kernel, devices), out_shape=pltpu....]
where the time goes in v5:
time: 35.4 us; the launch traced here: 35.3 us
  Pallas kernels  34.7 us (98%)
  local copies, waits for them, and re-layouts  0.63 us (2%)
    pallas_call x1, Pallas kernels, dense(): pl.pallas_call(functools.partial(layer_kernel, devices), out_shape=pltpu....  34.7 us

profile of v5, /device:TPU:0, one launch (start us, length us, event | category | flops | bytes accessed | tf_op | source)
XLA Modules:
  0.0 35.3 jit_solution(8784833179160360912)
XLA Ops:
  0.0 34.7 %shard_map.145 = bf16[8,4096]{1,0:T(8,128)(2,1)S(1)} custom-call(s32[16]{0:T(128)} %owners_hbm.1, s32[16]{0:T(128)} %lengths_hbm.1, s32[8]{0:T(128)} %blocks_hbm.1, bf16[16,2,16,256]{3,2,1,0:T(8,128)(2,1)} %bitcast.3, bf16[8,4096]{1,0:T(8,128)(2,1)} %q_hbm.1, bf16[8,2,256]{2,1,0:T(2,128)(2,1)} %dkv_hbm.1, s32[8,16]{1,0:T(8,128)} %table_hbm.1, ...), custom_call_target="tpu_custom_call" | custom-call | tf_op jit(solution)/shard_map/pallas_call | solution.py:926
  34.7 0.6 %copy.17 = bf16[8,4096]{1,0:T(8,128)(2,1)} copy(bf16[8,4096]{1,0:T(8,128)(2,1)S(1)} %shard_map.145) | data formatting | bytes 131072

commit v6 on v5

--- a/solution.py
+++ b/solution.py
@@ -697,7 +697,7 @@
         return ref[...].reshape(total, ref.shape[2])
 
     chunks = c_rsem.shape[1]
-    ends = (0, D // 4, D // 2, 3 * D // 4, D)
+    ends = (0, D // 4, 5 * D // 8, D)
 
     def cut(i):
         return slice(ends[i], ends[i + 1])
@@ -810,7 +810,7 @@
     def nothing():
         pass
 
-    behind = 2
+    behind = 1
     expert_rows(0, (finish_gather, nothing))
     expert_rows(1, (nothing, pass_b))
 
@@ -905,8 +905,8 @@
     lines = devices // 4
     chips = devices // 2
     bf16, f32 = jnp.bfloat16, jnp.float32
-    chunks = 4
-    pieces = 2
+    chunks = 3
+    pieces = 1
     b_chunks = 2
     packed = D * MAXP // seqs
     loaded = (

time: 35.4 us -> 35.5 us (level)
  no operation moved by 1% of the time
where the time goes in v6:
time: 35.5 us; the launch traced here: 35.4 us
  Pallas kernels  34.7 us (98%)
  local copies, waits for them, and re-layouts  0.63 us (2%)
    pallas_call x1, Pallas kernels, dense(): pl.pallas_call(functools.partial(layer_kernel, devices), out_shape=pltpu....  34.7 us

profile of v6, /device:TPU:0, one launch (start us, length us, event | category | flops | bytes accessed | tf_op | source)
XLA Modules:
  0.0 35.4 jit_solution(12329158694785446242)
XLA Ops:
  0.0 34.7 %shard_map.145 = bf16[8,4096]{1,0:T(8,128)(2,1)S(1)} custom-call(s32[16]{0:T(128)} %owners_hbm.1, s32[16]{0:T(128)} %lengths_hbm.1, s32[8]{0:T(128)} %blocks_hbm.1, bf16[16,2,16,256]{3,2,1,0:T(8,128)(2,1)} %bitcast.3, bf16[8,4096]{1,0:T(8,128)(2,1)} %q_hbm.1, bf16[8,2,256]{2,1,0:T(2,128)(2,1)} %dkv_hbm.1, s32[8,16]{1,0:T(8,128)} %table_hbm.1, ...), custom_call_target="tpu_custom_call" | custom-call | tf_op jit(solution)/shard_map/pallas_call | solution.py:926
  34.7 0.6 %copy.17 = bf16[8,4096]{1,0:T(8,128)(2,1)} copy(bf16[8,4096]{1,0:T(8,128)(2,1)S(1)} %shard_map.145) | data formatting | bytes 131072
